TPU v7x, 32 devices: a whole 2x2x4 slice. The times are simulated.
32 devices in a mesh: gx: 2 (over x), gy: 4 (over y, core), gz: 4 (over z).
Axes of the slice: x: 2, y: 2, z: 4, core: 2. Of those that a mesh axis runs over, the one named last changes fastest.
Arguments:
- right_side: float32 [24, 64, 512], P('gx', 'gy', 'gz'), may hold values from -8 to 8
- coefficient: float32 [24, 64, 512], P('gx', 'gy', 'gz'), may hold values from 0.02 to 1
Outputs:
- solution: float32 [24, 64, 512], P('gx', 'gy', 'gz')
- residual: float32 [24, 64, 512], P('gx', 'gy', 'gz')
- precond: float32 [24, 64, 512], P('gx', 'gy', 'gz')
- image: float32 [24, 64, 512], P('gx', 'gy', 'gz')
All inputs are finite; a program needn't handle non-finite values.
Results may differ from a plain program's by a relative error of at most 0.00021.
Values sent between devices are 32-bit elements; how exact they have to be, the bound alone decides.
A program may use at most 64 MiB of HBM per device.

v0:
```python
import jax
import jax.numpy as jnp
from jax import lax
from jax.sharding import PartitionSpec as P

SWEEPS = 4


relaxation = 0.6


def with_halo(block, sides, width):
    for axis, dim in sides:
        count = lax.axis_size(axis)
        forward = [(i, i + 1) for i in range(count - 1)]
        backward = [(target, source) for source, target in forward]
        low = lax.ppermute(
            lax.slice_in_dim(block, block.shape[dim] - width, None, axis=dim), axis, forward
        )
        high = lax.ppermute(lax.slice_in_dim(block, 0, width, axis=dim), axis, backward)
        block = jnp.concatenate([low, block, high], axis=dim)
    return block


def block_sum(padded):
    summed = padded[:-2] + padded[1:-1] + padded[2:]
    summed = summed[:, :-2] + summed[:, 1:-1] + summed[:, 2:]
    return summed[:, :, :-2] + summed[:, :, 1:-1] + summed[:, :, 2:]


def restrict(values):
    extent = values.shape
    grouped = values.reshape(extent[0] // 2, 2, extent[1] // 2, 2, extent[2] // 2, 2)
    return 0.5 * grouped.sum(axis=(1, 3, 5))


def prolong(values):
    return jnp.repeat(jnp.repeat(jnp.repeat(values, 2, axis=0), 2, axis=1), 2, axis=2)


def stencil(values, reaction):
    padded = with_halo(values, (("gx", 0), ("gy", 1), ("gz", 2)), 1)
    return (27.0 + reaction) * values - block_sum(padded)


def spread_deep(source, reaction):
    margin = SWEEPS - 1
    stacked = jnp.stack([source, reaction, jnp.ones_like(source)])
    widened = with_halo(stacked, (("gx", 1), ("gy", 2), ("gz", 3)), margin)
    wide_source = widened[0]
    wide_reaction = widened[1]
    inside = widened[2]
    correction = relaxation * wide_source / (26.0 + wide_reaction)
    for sweep in range(SWEEPS - 1):
        applied = (27.0 + wide_reaction) * correction - block_sum(jnp.pad(correction, 1))
        correction = (
            correction + relaxation * (wide_source - applied) / (26.0 + wide_reaction)
        ) * inside
    return correction[margin:-margin, margin:-margin, margin:-margin]


def coarsest(source, reaction):
    return spread_deep(source, reaction)


def multigrid(source, reactions, level_index):
    if level_index == 2:
        return coarsest(source, reactions[2])
    reaction = reactions[level_index]
    correction = relaxation * source / (26.0 + reaction)
    remainder = source - stencil(correction, reaction)
    correction = correction + prolong(multigrid(restrict(remainder), reactions, level_index + 1))
    return correction + relaxation * (source - stencil(correction, reaction)) / (26.0 + reaction)


def shards(right_side, coefficient):
    middle = restrict(coefficient)
    reactions = (coefficient, middle, restrict(middle))
    residual = right_side
    precond = multigrid(residual, reactions, 0)
    image = stencil(precond, coefficient)
    gamma_now, delta_now = lax.psum(
        (jnp.sum(residual * precond), jnp.sum(image * precond)), ("gx", "gy", "gz")
    )
    precond_image = multigrid(image, reactions, 0)
    image_twice = stencil(precond_image, coefficient)
    alpha_now = gamma_now / delta_now
    direction = precond
    dir_image = image
    solution = alpha_now * direction
    residual = residual - alpha_now * dir_image
    precond = precond - alpha_now * precond_image
    image = image - alpha_now * image_twice
    return (solution, residual, precond, image)


def solution(mesh):
    placed = (P("gx", "gy", "gz"), P("gx", "gy", "gz"))
    return jax.shard_map(
        shards,
        mesh=mesh,
        in_specs=placed,
        out_specs=(
            P("gx", "gy", "gz"),
            P("gx", "gy", "gz"),
            P("gx", "gy", "gz"),
            P("gx", "gy", "gz"),
        ),
        check_vma=False,
    )
```

profile of v0, /device:TPU:0, one launch (start us, length us, event | category | flops | bytes accessed | tf_op | source)
XLA Modules:
  0.0 375.8 jit_solution(6938410697397260277)
XLA Ops:
  1.6 4.9 %collective-permute-start = (f32[1,16,128]{2,1,0:T(8,128)S(1)}, f32[1,16,128]{2,1,0:T(8,128)S(1)}, u32[]{:S(2)}, u32[]{:S(2)}) collective-permute-start(f32[1,16,128]{2,1,0:T(8,128)S(1)} %get-tuple-element.98), channel_id=1, source_target_pairs={{0,16},{1,17},{2,18},{3,19},{4,20},{5,21},{6,22},{7,23},{8,24},{9,... | collective-permute-start | bytes 24584 | tf_op jit(solution)/shard_map/ppermute | solution.py:17
  7.8 4.2 %collective-permute-done.1 = f32[1,16,128]{2,1,0:T(8,128)S(1)} collective-permute-done((f32[1,16,128]{2,1,0:T(8,128)S(1)}, f32[1,16,128]{2,1,0:T(8,128)S(1)}, u32[]{:S(2)}, u32[]{:S(2)}) %collective-permute-start.1) | collective-permute-done | bytes 8224 | tf_op jit(solution)/shard_map/ppermute | solution.py:20
  14.7 3.5 collective-permute-done.3
  18.3 3.5 collective-permute-start.4
  23.1 8.4 %reshape.99 = f32[6,2,8,2,64,2]{5,4,3,2,1,0:T(8,128)} reshape(f32[12,16,128]{2,1,0:T(8,128)} %param.3) | data formatting | bytes 196608 | tf_op jit(solution)/shard_map/reshape | solution.py:33
  31.5 3.3 reduce_sum.73
  35.6 7.6 %reshape.98 = f32[6,2,8,2,64,2]{5,4,3,2,1,0:T(8,128)} reshape(f32[12,16,128]{2,1,0:T(8,128)S(1)} %fusion.37) | data formatting | bytes 196608 | tf_op jit(solution)/shard_map/reshape | solution.py:33
  43.3 3.3 reduce_sum.72
  49.5 4.2 %collective-permute-done.7 = f32[1,8,64]{2,1,0:T(8,128)S(1)} collective-permute-done((f32[1,8,64]{2,1,0:T(8,128)S(1)}, f32[1,8,64]{2,1,0:T(8,128)S(1)}, u32[]{:S(2)}, u32[]{:S(2)}) %collective-permute-start.7) | collective-permute-done | bytes 2080 | tf_op jit(solution)/shard_map/ppermute | solution.py:20
  53.7 2.6 collective-permute-start.8
  57.7 3.0 collective-permute-done.9
  60.7 4.5 %collective-permute-start.10 = (f32[8,10,1]{2,0,1:T(8,128)S(1)}, f32[8,10,1]{2,0,1:T(8,128)S(1)}, u32[]{:S(2)}, u32[]{:S(2)}) collective-permute-start(f32[8,10,1]{2,0,1:T(8,128)S(1)} %get-tuple-element.122), channel_id=1, source_target_pairs={{0,1},{1,2},{2,3},{4,5},{5,6},{6,7},{8,9},{9,10},{10,11},{12,13},{... | collective-permute-start | bytes 968 | tf_op jit(solution)/shard_map/ppermute | solution.py:17
  66.9 4.2 %collective-permute-done.11 = f32[8,10,1]{2,0,1:T(8,128)S(1)} collective-permute-done((f32[8,10,1]{2,0,1:T(8,128)S(1)}, f32[8,10,1]{2,0,1:T(8,128)S(1)}, u32[]{:S(2)}, u32[]{:S(2)}) %collective-permute-start.11) | collective-permute-done | bytes 352 | tf_op jit(solution)/shard_map/ppermute | solution.py:20
  74.7 4.5 %collective-permute-start.12 = (f32[3,3,4,32]{3,2,1,0:T(4,128)S(1)}, f32[3,3,4,32]{3,2,1,0:T(4,128)S(1)}, u32[]{:S(2)}, u32[]{:S(2)}) collective-permute-start(f32[3,3,4,32]{3,2,1,0:T(4,128)S(1)} %pad_maximum_fusion.37), channel_id=1, source_target_pairs={{0,16},{1,17},{2,18},{3,19},{4,20},{5,21},{6,22},{7,23},{8,24},{9,... | collective-permute-start | bytes 13832 | tf_op jit(solution)/shard_map/ppermute | solution.py:17
  80.7 1.7 collective-permute-start.14
  83.7 3.9 %collective-permute-done.15 = f32[3,9,3,32]{3,2,1,0:T(4,128)S(1)} collective-permute-done((f32[3,9,3,32]{3,2,1,0:T(4,128)S(1)}, f32[3,9,3,32]{3,2,1,0:T(4,128)S(1)}, u32[]{:S(2)}, u32[]{:S(2)}) %collective-permute-start.15) | collective-permute-done | bytes 10400 | tf_op jit(solution)/shard_map/ppermute | solution.py:20
  87.9 3.5 collective-permute-start.16
  92.7 2.6 collective-permute-done.16
  95.3 4.7 %collective-permute-done.17 = f32[3,9,10,3]{3,2,1,0:T(8,128)S(1)} collective-permute-done((f32[3,9,10,3]{3,2,1,0:T(8,128)S(1)}, f32[3,9,10,3]{3,2,1,0:T(8,128)S(1)}, u32[]{:S(2)}, u32[]{:S(2)}) %collective-permute-start.17) | collective-permute-done | bytes 3272 | tf_op jit(solution)/shard_map/ppermute | solution.py:20
  101.5 4.2 %collective-permute-start.18 = (f32[1,8,64]{2,1,0:T(8,128)S(1)}, f32[1,8,64]{2,1,0:T(8,128)S(1)}, u32[]{:S(2)}, u32[]{:S(2)}) collective-permute-start(f32[1,8,64]{2,1,0:T(8,128)S(1)} %get-tuple-element.136), channel_id=1, source_target_pairs={{0,16},{1,17},{2,18},{3,19},{4,20},{5,21},{6,22},{7,23},{8,24},{9,... | collective-permute-start | bytes 6152 | tf_op jit(solution)/shard_map/ppermute | solution.py:17
  107.1 4.2 %collective-permute-done.19 = f32[1,8,64]{2,1,0:T(8,128)S(1)} collective-permute-done((f32[1,8,64]{2,1,0:T(8,128)S(1)}, f32[1,8,64]{2,1,0:T(8,128)S(1)}, u32[]{:S(2)}, u32[]{:S(2)}) %collective-permute-start.19) | collective-permute-done | bytes 2080 | tf_op jit(solution)/shard_map/ppermute | solution.py:20
  111.3 2.0 collective-permute-start.20
  114.6 3.2 collective-permute-done.21
  117.9 3.5 collective-permute-start.22
  123.0 4.2 %collective-permute-done.23 = f32[8,10,1]{2,0,1:T(8,128)S(1)} collective-permute-done((f32[8,10,1]{2,0,1:T(8,128)S(1)}, f32[8,10,1]{2,0,1:T(8,128)S(1)}, u32[]{:S(2)}, u32[]{:S(2)}) %collective-permute-start.23) | collective-permute-done | bytes 352 | tf_op jit(solution)/shard_map/ppermute | solution.py:20
  131.3 4.2 %collective-permute-done.25 = f32[1,16,128]{2,1,0:T(8,128)S(1)} collective-permute-done((f32[1,16,128]{2,1,0:T(8,128)S(1)}, f32[1,16,128]{2,1,0:T(8,128)S(1)}, u32[]{:S(2)}, u32[]{:S(2)}) %collective-permute-start.25) | collective-permute-done | bytes 8224 | tf_op jit(solution)/shard_map/ppermute | solution.py:20
  138.3 4.1 %collective-permute-done.27 = f32[14,1,128]{2,1,0:T(1,128)S(1)} collective-permute-done((f32[14,1,128]{2,1,0:T(1,128)S(1)}, f32[14,1,128]{2,1,0:T(1,128)S(1)}, u32[]{:S(2)}, u32[]{:S(2)}) %collective-permute-start.27) | collective-permute-done | bytes 7200 | tf_op jit(solution)/shard_map/ppermute | solution.py:20
  142.5 1.9 collective-permute-start.28
  147.2 4.7 %collective-permute-done.29 = f32[14,18,1]{2,0,1:T(8,128)S(1)} collective-permute-done((f32[14,18,1]{2,0,1:T(8,128)S(1)}, f32[14,18,1]{2,0,1:T(8,128)S(1)}, u32[]{:S(2)}, u32[]{:S(2)}) %collective-permute-start.29) | collective-permute-done | bytes 1040 | tf_op jit(solution)/shard_map/ppermute | solution.py:20
  155.8 4.2 %collective-permute-done.31 = f32[1,16,128]{2,1,0:T(8,128)S(1)} collective-permute-done((f32[1,16,128]{2,1,0:T(8,128)S(1)}, f32[1,16,128]{2,1,0:T(8,128)S(1)}, u32[]{:S(2)}, u32[]{:S(2)}) %collective-permute-start.31) | collective-permute-done | bytes 8224 | tf_op jit(solution)/shard_map/ppermute | solution.py:20
  162.8 3.7 collective-permute-done.33
  166.6 1.9 collective-permute-start.34
  171.3 4.7 %collective-permute-done.35 = f32[14,18,1]{2,0,1:T(8,128)S(1)} collective-permute-done((f32[14,18,1]{2,0,1:T(8,128)S(1)}, f32[14,18,1]{2,0,1:T(8,128)S(1)}, u32[]{:S(2)}, u32[]{:S(2)}) %collective-permute-start.35) | collective-permute-done | bytes 1040 | tf_op jit(solution)/shard_map/ppermute | solution.py:20
  179.9 4.2 %collective-permute-done.37 = f32[1,16,128]{2,1,0:T(8,128)S(1)} collective-permute-done((f32[1,16,128]{2,1,0:T(8,128)S(1)}, f32[1,16,128]{2,1,0:T(8,128)S(1)}, u32[]{:S(2)}, u32[]{:S(2)}) %collective-permute-start.37) | collective-permute-done | bytes 8224 | tf_op jit(solution)/shard_map/ppermute | solution.py:20
  187.0 3.7 collective-permute-done.39
  190.8 1.9 collective-permute-start.40
  195.5 4.7 %collective-permute-done.41 = f32[14,18,1]{2,0,1:T(8,128)S(1)} collective-permute-done((f32[14,18,1]{2,0,1:T(8,128)S(1)}, f32[14,18,1]{2,0,1:T(8,128)S(1)}, u32[]{:S(2)}, u32[]{:S(2)}) %collective-permute-start.41) | collective-permute-done | bytes 1040 | tf_op jit(solution)/shard_map/ppermute | solution.py:20
  201.0 7.6 %reshape.107 = f32[6,2,8,2,64,2]{5,4,3,2,1,0:T(8,128)} reshape(f32[12,16,128]{2,1,0:T(8,128)S(1)} %fusion.29) | data formatting | bytes 196608 | tf_op jit(solution)/shard_map/reshape | solution.py:33
  208.6 3.3 reduce_sum.78
  214.9 4.2 %collective-permute-done.43 = f32[1,8,64]{2,1,0:T(8,128)S(1)} collective-permute-done((f32[1,8,64]{2,1,0:T(8,128)S(1)}, f32[1,8,64]{2,1,0:T(8,128)S(1)}, u32[]{:S(2)}, u32[]{:S(2)}) %collective-permute-start.43) | collective-permute-done | bytes 2080 | tf_op jit(solution)/shard_map/ppermute | solution.py:20
  221.9 3.7 collective-permute-done.45
  225.7 1.9 collective-permute-start.46
  229.3 4.2 %collective-permute-done.47 = f32[8,10,1]{2,0,1:T(8,128)S(1)} collective-permute-done((f32[8,10,1]{2,0,1:T(8,128)S(1)}, f32[8,10,1]{2,0,1:T(8,128)S(1)}, u32[]{:S(2)}, u32[]{:S(2)}) %collective-permute-start.47) | collective-permute-done | bytes 352 | tf_op jit(solution)/shard_map/ppermute | solution.py:20
  236.0 4.5 %collective-permute-start.48 = (f32[3,3,4,32]{3,2,1,0:T(4,128)S(1)}, f32[3,3,4,32]{3,2,1,0:T(4,128)S(1)}, u32[]{:S(2)}, u32[]{:S(2)}) collective-permute-start(f32[3,3,4,32]{3,2,1,0:T(4,128)S(1)} %pad_maximum_fusion.36), channel_id=1, source_target_pairs={{0,16},{1,17},{2,18},{3,19},{4,20},{5,21},{6,22},{7,23},{8,24},{9,... | collective-permute-start | bytes 13832 | tf_op jit(solution)/shard_map/ppermute | solution.py:17
  242.1 1.7 collective-permute-start.50
  245.1 3.9 %collective-permute-done.51 = f32[3,9,3,32]{3,2,1,0:T(4,128)S(1)} collective-permute-done((f32[3,9,3,32]{3,2,1,0:T(4,128)S(1)}, f32[3,9,3,32]{3,2,1,0:T(4,128)S(1)}, u32[]{:S(2)}, u32[]{:S(2)}) %collective-permute-start.51) | collective-permute-done | bytes 10400 | tf_op jit(solution)/shard_map/ppermute | solution.py:20
  249.2 1.9 collective-permute-start.52
  252.5 2.6 collective-permute-done.52
  255.1 4.7 %collective-permute-done.53 = f32[3,9,10,3]{3,2,1,0:T(8,128)S(1)} collective-permute-done((f32[3,9,10,3]{3,2,1,0:T(8,128)S(1)}, f32[3,9,10,3]{3,2,1,0:T(8,128)S(1)}, u32[]{:S(2)}, u32[]{:S(2)}) %collective-permute-start.53) | collective-permute-done | bytes 3272 | tf_op jit(solution)/shard_map/ppermute | solution.py:20
  261.3 4.2 %collective-permute-start.54 = (f32[1,8,64]{2,1,0:T(8,128)S(1)}, f32[1,8,64]{2,1,0:T(8,128)S(1)}, u32[]{:S(2)}, u32[]{:S(2)}) collective-permute-start(f32[1,8,64]{2,1,0:T(8,128)S(1)} %get-tuple-element.132), channel_id=1, source_target_pairs={{0,16},{1,17},{2,18},{3,19},{4,20},{5,21},{6,22},{7,23},{8,24},{9,... | collective-permute-start | bytes 6152 | tf_op jit(solution)/shard_map/ppermute | solution.py:17
  266.9 4.2 %collective-permute-done.55 = f32[1,8,64]{2,1,0:T(8,128)S(1)} collective-permute-done((f32[1,8,64]{2,1,0:T(8,128)S(1)}, f32[1,8,64]{2,1,0:T(8,128)S(1)}, u32[]{:S(2)}, u32[]{:S(2)}) %collective-permute-start.55) | collective-permute-done | bytes 2080 | tf_op jit(solution)/shard_map/ppermute | solution.py:20
  271.1 2.0 collective-permute-start.56
  274.4 3.2 collective-permute-done.57
  277.7 1.9 collective-permute-start.58
  281.2 4.2 %collective-permute-done.59 = f32[8,10,1]{2,0,1:T(8,128)S(1)} collective-permute-done((f32[8,10,1]{2,0,1:T(8,128)S(1)}, f32[8,10,1]{2,0,1:T(8,128)S(1)}, u32[]{:S(2)}, u32[]{:S(2)}) %collective-permute-start.59) | collective-permute-done | bytes 352 | tf_op jit(solution)/shard_map/ppermute | solution.py:20
  290.1 4.2 %collective-permute-done.61 = f32[1,16,128]{2,1,0:T(8,128)S(1)} collective-permute-done((f32[1,16,128]{2,1,0:T(8,128)S(1)}, f32[1,16,128]{2,1,0:T(8,128)S(1)}, u32[]{:S(2)}, u32[]{:S(2)}) %collective-permute-start.61) | collective-permute-done | bytes 8224 | tf_op jit(solution)/shard_map/ppermute | solution.py:20
  297.1 4.1 %collective-permute-done.63 = f32[14,1,128]{2,1,0:T(1,128)S(1)} collective-permute-done((f32[14,1,128]{2,1,0:T(1,128)S(1)}, f32[14,1,128]{2,1,0:T(1,128)S(1)}, u32[]{:S(2)}, u32[]{:S(2)}) %collective-permute-start.63) | collective-permute-done | bytes 7200 | tf_op jit(solution)/shard_map/ppermute | solution.py:20
  301.3 1.9 collective-permute-start.64
  304.6 41.1 %all-reduce.6 = (f32[]{:T(128)}, f32[]{:T(128)}) all-reduce(f32[]{:T(128)} %get-tuple-element.21, f32[]{:T(128)} %get-tuple-element.20), channel_id=1, replica_groups=mesh['gx'=2,'gy'=4,'gz'=4] {'gx','gy','gz'}, use_global_device_ids=true, to_apply=%region_5.6 | all-reduce | flops 2 | bytes 16 | tf_op jit(solution)/shard_map/psum | solution.py:82
  348.5 4.2 %collective-permute-start.66 = (f32[1,16,128]{2,1,0:T(8,128)S(1)}, f32[1,16,128]{2,1,0:T(8,128)S(1)}, u32[]{:S(2)}, u32[]{:S(2)}) collective-permute-start(f32[1,16,128]{2,1,0:T(8,128)S(1)} %get-tuple-element.86), channel_id=1, source_target_pairs={{0,16},{1,17},{2,18},{3,19},{4,20},{5,21},{6,22},{7,23},{8,24},{9,... | collective-permute-start | bytes 24584 | tf_op jit(solution)/shard_map/ppermute | solution.py:17
  354.0 4.2 %collective-permute-done.67 = f32[1,16,128]{2,1,0:T(8,128)S(1)} collective-permute-done((f32[1,16,128]{2,1,0:T(8,128)S(1)}, f32[1,16,128]{2,1,0:T(8,128)S(1)}, u32[]{:S(2)}, u32[]{:S(2)}) %collective-permute-start.67) | collective-permute-done | bytes 8224 | tf_op jit(solution)/shard_map/ppermute | solution.py:20
  360.9 4.0 %collective-permute-done.69 = f32[14,1,128]{2,1,0:T(1,128)S(1)} collective-permute-done((f32[14,1,128]{2,1,0:T(1,128)S(1)}, f32[14,1,128]{2,1,0:T(1,128)S(1)}, u32[]{:S(2)}, u32[]{:S(2)}) %collective-permute-start.69) | collective-permute-done | bytes 7200 | tf_op jit(solution)/shard_map/ppermute | solution.py:20
  365.0 1.8 collective-permute-start.70
  369.6 4.7 %collective-permute-done.71 = f32[14,18,1]{2,0,1:T(8,128)S(1)} collective-permute-done((f32[14,18,1]{2,0,1:T(8,128)S(1)}, f32[14,18,1]{2,0,1:T(8,128)S(1)}, u32[]{:S(2)}, u32[]{:S(2)}) %collective-permute-start.71) | collective-permute-done | bytes 1040 | tf_op jit(solution)/shard_map/ppermute | solution.py:20
  (279 shorter events, 94.4 us)
Async XLA Ops:
  1.6 6.2 %collective-permute-start = (f32[1,16,128]{2,1,0:T(8,128)S(1)}, f32[1,16,128]{2,1,0:T(8,128)S(1)}, u32[]{:S(2)}, u32[]{:S(2)}) collective-permute-start(f32[1,16,128]{2,1,0:T(8,128)S(1)} %get-tuple-element.98), channel_id=1, source_target_pairs={{0,16},{1,17},{2,18},{3,19},{4,20},{5,21},{6,22},{7,23},{8,24},{9,... | collective-permute-start | bytes 24584 | tf_op jit(solution)/shard_map/ppermute | solution.py:17
  6.5 5.5 %collective-permute-start.1 = (f32[1,16,128]{2,1,0:T(8,128)S(1)}, f32[1,16,128]{2,1,0:T(8,128)S(1)}, u32[]{:S(2)}, u32[]{:S(2)}) collective-permute-start(f32[1,16,128]{2,1,0:T(8,128)S(1)} %get-tuple-element.99), channel_id=1, source_target_pairs={{16,0},{17,1},{18,2},{19,3},{20,4},{21,5},{22,6},{23,7},{24,8},{25... | collective-permute-start | bytes 24584 | tf_op jit(solution)/shard_map/ppermute | solution.py:20
  13.4 4.8 %collective-permute-start.3 = (f32[14,1,128]{2,1,0:T(1,128)S(1)}, f32[14,1,128]{2,1,0:T(1,128)S(1)}, u32[]{:S(2)}, u32[]{:S(2)}) collective-permute-start(f32[14,1,128]{2,1,0:T(1,128)S(1)} %get-tuple-element.82), channel_id=1, source_target_pairs={{4,0},{8,4},{12,8},{5,1},{9,5},{13,9},{6,2},{10,6},{14,10},{7,3},{... | collective-permute-start | bytes 21512 | tf_op jit(solution)/shard_map/ppermute | solution.py:20
  18.3 16.5 %collective-permute-start.4 = (f32[14,18,1]{2,0,1:T(8,128)S(1)}, f32[14,18,1]{2,0,1:T(8,128)S(1)}, u32[]{:S(2)}, u32[]{:S(2)}) collective-permute-start(f32[14,18,1]{2,0,1:T(8,128)S(1)} %get-tuple-element.70), channel_id=1, source_target_pairs={{0,1},{1,2},{2,3},{4,5},{5,6},{6,7},{8,9},{9,10},{10,11},{12,13},{... | collective-permute-start | bytes 3032 | tf_op jit(solution)/shard_map/ppermute | solution.py:17
  21.8 13.0 %collective-permute-start.5 = (f32[14,18,1]{2,0,1:T(8,128)S(1)}, f32[14,18,1]{2,0,1:T(8,128)S(1)}, u32[]{:S(2)}, u32[]{:S(2)}) collective-permute-start(f32[14,18,1]{2,0,1:T(8,128)S(1)} %get-tuple-element.71), channel_id=1, source_target_pairs={{1,0},{2,1},{3,2},{5,4},{6,5},{7,6},{9,8},{10,9},{11,10},{13,12},{... | collective-permute-start | bytes 3032 | tf_op jit(solution)/shard_map/ppermute | solution.py:20
  46.6 3.0 collective-permute-start.6
  48.2 5.5 %collective-permute-start.7 = (f32[1,8,64]{2,1,0:T(8,128)S(1)}, f32[1,8,64]{2,1,0:T(8,128)S(1)}, u32[]{:S(2)}, u32[]{:S(2)}) collective-permute-start(f32[1,8,64]{2,1,0:T(8,128)S(1)} %get-tuple-element.141), channel_id=1, source_target_pairs={{16,0},{17,1},{18,2},{19,3},{20,4},{21,5},{22,6},{23,7},{24,8},{25... | collective-permute-start | bytes 6152 | tf_op jit(solution)/shard_map/ppermute | solution.py:20
  53.7 3.9 %collective-permute-start.8 = (f32[8,1,64]{2,1,0:T(1,128)S(1)}, f32[8,1,64]{2,1,0:T(1,128)S(1)}, u32[]{:S(2)}, u32[]{:S(2)}) collective-permute-start(f32[8,1,64]{2,1,0:T(1,128)S(1)} %get-tuple-element.130), channel_id=1, source_target_pairs={{0,4},{4,8},{8,12},{1,5},{5,9},{9,13},{2,6},{6,10},{10,14},{3,7},{... | collective-permute-start | bytes 6152 | tf_op jit(solution)/shard_map/ppermute | solution.py:17
  56.3 4.3 %collective-permute-start.9 = (f32[8,1,64]{2,1,0:T(1,128)S(1)}, f32[8,1,64]{2,1,0:T(1,128)S(1)}, u32[]{:S(2)}, u32[]{:S(2)}) collective-permute-start(f32[8,1,64]{2,1,0:T(1,128)S(1)} %get-tuple-element.131), channel_id=1, source_target_pairs={{4,0},{8,4},{12,8},{5,1},{9,5},{13,9},{6,2},{10,6},{14,10},{7,3},{... | collective-permute-start | bytes 6152 | tf_op jit(solution)/shard_map/ppermute | solution.py:20
  60.7 6.2 %collective-permute-start.10 = (f32[8,10,1]{2,0,1:T(8,128)S(1)}, f32[8,10,1]{2,0,1:T(8,128)S(1)}, u32[]{:S(2)}, u32[]{:S(2)}) collective-permute-start(f32[8,10,1]{2,0,1:T(8,128)S(1)} %get-tuple-element.122), channel_id=1, source_target_pairs={{0,1},{1,2},{2,3},{4,5},{5,6},{6,7},{8,9},{9,10},{10,11},{12,13},{... | collective-permute-start | bytes 968 | tf_op jit(solution)/shard_map/ppermute | solution.py:17
  65.3 5.9 %collective-permute-start.11 = (f32[8,10,1]{2,0,1:T(8,128)S(1)}, f32[8,10,1]{2,0,1:T(8,128)S(1)}, u32[]{:S(2)}, u32[]{:S(2)}) collective-permute-start(f32[8,10,1]{2,0,1:T(8,128)S(1)} %get-tuple-element.123), channel_id=1, source_target_pairs={{1,0},{2,1},{3,2},{5,4},{6,5},{7,6},{9,8},{10,9},{11,10},{13,12},{... | collective-permute-start | bytes 968 | tf_op jit(solution)/shard_map/ppermute | solution.py:20
  73.4 5.9 %collective-permute-start.13 = (f32[3,3,4,32]{3,2,1,0:T(4,128)S(1)}, f32[3,3,4,32]{3,2,1,0:T(4,128)S(1)}, u32[]{:S(2)}, u32[]{:S(2)}) collective-permute-start(f32[3,3,4,32]{3,2,1,0:T(4,128)S(1)} %pad_maximum_fusion.37), channel_id=1, source_target_pairs={{16,0},{17,1},{18,2},{19,3},{20,4},{21,5},{22,6},{23,7},{24,8},{25... | collective-permute-start | bytes 13832 | tf_op jit(solution)/shard_map/ppermute | solution.py:20
  74.7 6.0 %collective-permute-start.12 = (f32[3,3,4,32]{3,2,1,0:T(4,128)S(1)}, f32[3,3,4,32]{3,2,1,0:T(4,128)S(1)}, u32[]{:S(2)}, u32[]{:S(2)}) collective-permute-start(f32[3,3,4,32]{3,2,1,0:T(4,128)S(1)} %pad_maximum_fusion.37), channel_id=1, source_target_pairs={{0,16},{1,17},{2,18},{3,19},{4,20},{5,21},{6,22},{7,23},{8,24},{9,... | collective-permute-start | bytes 13832 | tf_op jit(solution)/shard_map/ppermute | solution.py:17
  80.7 3.0 collective-permute-start.14
  82.4 5.2 %collective-permute-start.15 = (f32[3,9,3,32]{3,2,1,0:T(4,128)S(1)}, f32[3,9,3,32]{3,2,1,0:T(4,128)S(1)}, u32[]{:S(2)}, u32[]{:S(2)}) collective-permute-start(f32[3,9,3,32]{3,2,1,0:T(4,128)S(1)} %get-tuple-element.103), channel_id=1, source_target_pairs={{4,0},{8,4},{12,8},{5,1},{9,5},{13,9},{6,2},{10,6},{14,10},{7,3},{... | collective-permute-start | bytes 31112 | tf_op jit(solution)/shard_map/ppermute | solution.py:20
  87.9 7.4 %collective-permute-start.16 = (f32[3,9,10,3]{3,2,1,0:T(8,128)S(1)}, f32[3,9,10,3]{3,2,1,0:T(8,128)S(1)}, u32[]{:S(2)}, u32[]{:S(2)}) collective-permute-start(f32[3,9,10,3]{3,2,1,0:T(8,128)S(1)} %get-tuple-element.58), channel_id=1, source_target_pairs={{0,1},{1,2},{2,3},{4,5},{5,6},{6,7},{8,9},{9,10},{10,11},{12,13},{... | collective-permute-start | bytes 9728 | tf_op jit(solution)/shard_map/ppermute | solution.py:17
  91.4 8.6 %collective-permute-start.17 = (f32[3,9,10,3]{3,2,1,0:T(8,128)S(1)}, f32[3,9,10,3]{3,2,1,0:T(8,128)S(1)}, u32[]{:S(2)}, u32[]{:S(2)}) collective-permute-start(f32[3,9,10,3]{3,2,1,0:T(8,128)S(1)} %get-tuple-element.59), channel_id=1, source_target_pairs={{1,0},{2,1},{3,2},{5,4},{6,5},{7,6},{9,8},{10,9},{11,10},{13,12},{... | collective-permute-start | bytes 9728 | tf_op jit(solution)/shard_map/ppermute | solution.py:20
  101.5 5.5 %collective-permute-start.18 = (f32[1,8,64]{2,1,0:T(8,128)S(1)}, f32[1,8,64]{2,1,0:T(8,128)S(1)}, u32[]{:S(2)}, u32[]{:S(2)}) collective-permute-start(f32[1,8,64]{2,1,0:T(8,128)S(1)} %get-tuple-element.136), channel_id=1, source_target_pairs={{0,16},{1,17},{2,18},{3,19},{4,20},{5,21},{6,22},{7,23},{8,24},{9,... | collective-permute-start | bytes 6152 | tf_op jit(solution)/shard_map/ppermute | solution.py:17
  105.8 5.5 %collective-permute-start.19 = (f32[1,8,64]{2,1,0:T(8,128)S(1)}, f32[1,8,64]{2,1,0:T(8,128)S(1)}, u32[]{:S(2)}, u32[]{:S(2)}) collective-permute-start(f32[1,8,64]{2,1,0:T(8,128)S(1)} %get-tuple-element.137), channel_id=1, source_target_pairs={{16,0},{17,1},{18,2},{19,3},{20,4},{21,5},{22,6},{23,7},{24,8},{25... | collective-permute-start | bytes 6152 | tf_op jit(solution)/shard_map/ppermute | solution.py:20
  111.3 3.3 collective-permute-start.20
  113.3 4.5 %collective-permute-start.21 = (f32[8,1,64]{2,1,0:T(1,128)S(1)}, f32[8,1,64]{2,1,0:T(1,128)S(1)}, u32[]{:S(2)}, u32[]{:S(2)}) collective-permute-start(f32[8,1,64]{2,1,0:T(1,128)S(1)} %get-tuple-element.129), channel_id=1, source_target_pairs={{4,0},{8,4},{12,8},{5,1},{9,5},{13,9},{6,2},{10,6},{14,10},{7,3},{... | collective-permute-start | bytes 6152 | tf_op jit(solution)/shard_map/ppermute | solution.py:20
  117.9 5.1 %collective-permute-start.22 = (f32[8,10,1]{2,0,1:T(8,128)S(1)}, f32[8,10,1]{2,0,1:T(8,128)S(1)}, u32[]{:S(2)}, u32[]{:S(2)}) collective-permute-start(f32[8,10,1]{2,0,1:T(8,128)S(1)} %get-tuple-element.117), channel_id=1, source_target_pairs={{0,1},{1,2},{2,3},{4,5},{5,6},{6,7},{8,9},{9,10},{10,11},{12,13},{... | collective-permute-start | bytes 968 | tf_op jit(solution)/shard_map/ppermute | solution.py:17
  121.3 5.9 %collective-permute-start.23 = (f32[8,10,1]{2,0,1:T(8,128)S(1)}, f32[8,10,1]{2,0,1:T(8,128)S(1)}, u32[]{:S(2)}, u32[]{:S(2)}) collective-permute-start(f32[8,10,1]{2,0,1:T(8,128)S(1)} %get-tuple-element.118), channel_id=1, source_target_pairs={{1,0},{2,1},{3,2},{5,4},{6,5},{7,6},{9,8},{10,9},{11,10},{13,12},{... | collective-permute-start | bytes 968 | tf_op jit(solution)/shard_map/ppermute | solution.py:20
  128.3 3.0 collective-permute-start.24
  129.9 5.5 %collective-permute-start.25 = (f32[1,16,128]{2,1,0:T(8,128)S(1)}, f32[1,16,128]{2,1,0:T(8,128)S(1)}, u32[]{:S(2)}, u32[]{:S(2)}) collective-permute-start(f32[1,16,128]{2,1,0:T(8,128)S(1)} %get-tuple-element.97), channel_id=1, source_target_pairs={{16,0},{17,1},{18,2},{19,3},{20,4},{21,5},{22,6},{23,7},{24,8},{25... | collective-permute-start | bytes 24584 | tf_op jit(solution)/shard_map/ppermute | solution.py:20
  136.9 5.5 %collective-permute-start.27 = (f32[14,1,128]{2,1,0:T(1,128)S(1)}, f32[14,1,128]{2,1,0:T(1,128)S(1)}, u32[]{:S(2)}, u32[]{:S(2)}) collective-permute-start(f32[14,1,128]{2,1,0:T(1,128)S(1)} %get-tuple-element.80), channel_id=1, source_target_pairs={{4,0},{8,4},{12,8},{5,1},{9,5},{13,9},{6,2},{10,6},{14,10},{7,3},{... | collective-permute-start | bytes 21512 | tf_op jit(solution)/shard_map/ppermute | solution.py:20
  142.5 4.7 %collective-permute-start.28 = (f32[14,18,1]{2,0,1:T(8,128)S(1)}, f32[14,18,1]{2,0,1:T(8,128)S(1)}, u32[]{:S(2)}, u32[]{:S(2)}) collective-permute-start(f32[14,18,1]{2,0,1:T(8,128)S(1)} %get-tuple-element.68), channel_id=1, source_target_pairs={{0,1},{1,2},{2,3},{4,5},{5,6},{6,7},{8,9},{9,10},{10,11},{12,13},{... | collective-permute-start | bytes 3032 | tf_op jit(solution)/shard_map/ppermute | solution.py:17
  144.5 7.5 %collective-permute-start.29 = (f32[14,18,1]{2,0,1:T(8,128)S(1)}, f32[14,18,1]{2,0,1:T(8,128)S(1)}, u32[]{:S(2)}, u32[]{:S(2)}) collective-permute-start(f32[14,18,1]{2,0,1:T(8,128)S(1)} %get-tuple-element.69), channel_id=1, source_target_pairs={{1,0},{2,1},{3,2},{5,4},{6,5},{7,6},{9,8},{10,9},{11,10},{13,12},{... | collective-permute-start | bytes 3032 | tf_op jit(solution)/shard_map/ppermute | solution.py:20
  152.8 3.0 collective-permute-start.30
  154.4 5.5 %collective-permute-start.31 = (f32[1,16,128]{2,1,0:T(8,128)S(1)}, f32[1,16,128]{2,1,0:T(8,128)S(1)}, u32[]{:S(2)}, u32[]{:S(2)}) collective-permute-start(f32[1,16,128]{2,1,0:T(8,128)S(1)} %get-tuple-element.95), channel_id=1, source_target_pairs={{16,0},{17,1},{18,2},{19,3},{20,4},{21,5},{22,6},{23,7},{24,8},{25... | collective-permute-start | bytes 24584 | tf_op jit(solution)/shard_map/ppermute | solution.py:20
  161.4 5.0 %collective-permute-start.33 = (f32[14,1,128]{2,1,0:T(1,128)S(1)}, f32[14,1,128]{2,1,0:T(1,128)S(1)}, u32[]{:S(2)}, u32[]{:S(2)}) collective-permute-start(f32[14,1,128]{2,1,0:T(1,128)S(1)} %get-tuple-element.78), channel_id=1, source_target_pairs={{4,0},{8,4},{12,8},{5,1},{9,5},{13,9},{6,2},{10,6},{14,10},{7,3},{... | collective-permute-start | bytes 21512 | tf_op jit(solution)/shard_map/ppermute | solution.py:20
  166.6 4.7 %collective-permute-start.34 = (f32[14,18,1]{2,0,1:T(8,128)S(1)}, f32[14,18,1]{2,0,1:T(8,128)S(1)}, u32[]{:S(2)}, u32[]{:S(2)}) collective-permute-start(f32[14,18,1]{2,0,1:T(8,128)S(1)} %get-tuple-element.66), channel_id=1, source_target_pairs={{0,1},{1,2},{2,3},{4,5},{5,6},{6,7},{8,9},{9,10},{10,11},{12,13},{... | collective-permute-start | bytes 3032 | tf_op jit(solution)/shard_map/ppermute | solution.py:17
  168.5 7.5 %collective-permute-start.35 = (f32[14,18,1]{2,0,1:T(8,128)S(1)}, f32[14,18,1]{2,0,1:T(8,128)S(1)}, u32[]{:S(2)}, u32[]{:S(2)}) collective-permute-start(f32[14,18,1]{2,0,1:T(8,128)S(1)} %get-tuple-element.67), channel_id=1, source_target_pairs={{1,0},{2,1},{3,2},{5,4},{6,5},{7,6},{9,8},{10,9},{11,10},{13,12},{... | collective-permute-start | bytes 3032 | tf_op jit(solution)/shard_map/ppermute | solution.py:20
  176.8 3.1 collective-permute-start.36
  178.5 5.7 %collective-permute-start.37 = (f32[1,16,128]{2,1,0:T(8,128)S(1)}, f32[1,16,128]{2,1,0:T(8,128)S(1)}, u32[]{:S(2)}, u32[]{:S(2)}) collective-permute-start(f32[1,16,128]{2,1,0:T(8,128)S(1)} %get-tuple-element.93), channel_id=1, source_target_pairs={{16,0},{17,1},{18,2},{19,3},{20,4},{21,5},{22,6},{23,7},{24,8},{25... | collective-permute-start | bytes 24584 | tf_op jit(solution)/shard_map/ppermute | solution.py:20
  185.7 5.0 %collective-permute-start.39 = (f32[14,1,128]{2,1,0:T(1,128)S(1)}, f32[14,1,128]{2,1,0:T(1,128)S(1)}, u32[]{:S(2)}, u32[]{:S(2)}) collective-permute-start(f32[14,1,128]{2,1,0:T(1,128)S(1)} %get-tuple-element.76), channel_id=1, source_target_pairs={{4,0},{8,4},{12,8},{5,1},{9,5},{13,9},{6,2},{10,6},{14,10},{7,3},{... | collective-permute-start | bytes 21512 | tf_op jit(solution)/shard_map/ppermute | solution.py:20
  190.8 4.7 %collective-permute-start.40 = (f32[14,18,1]{2,0,1:T(8,128)S(1)}, f32[14,18,1]{2,0,1:T(8,128)S(1)}, u32[]{:S(2)}, u32[]{:S(2)}) collective-permute-start(f32[14,18,1]{2,0,1:T(8,128)S(1)} %get-tuple-element.64), channel_id=1, source_target_pairs={{0,1},{1,2},{2,3},{4,5},{5,6},{6,7},{8,9},{9,10},{10,11},{12,13},{... | collective-permute-start | bytes 3032 | tf_op jit(solution)/shard_map/ppermute | solution.py:17
  192.7 7.5 %collective-permute-start.41 = (f32[14,18,1]{2,0,1:T(8,128)S(1)}, f32[14,18,1]{2,0,1:T(8,128)S(1)}, u32[]{:S(2)}, u32[]{:S(2)}) collective-permute-start(f32[14,18,1]{2,0,1:T(8,128)S(1)} %get-tuple-element.65), channel_id=1, source_target_pairs={{1,0},{2,1},{3,2},{5,4},{6,5},{7,6},{9,8},{10,9},{11,10},{13,12},{... | collective-permute-start | bytes 3032 | tf_op jit(solution)/shard_map/ppermute | solution.py:20
  213.6 5.5 %collective-permute-start.43 = (f32[1,8,64]{2,1,0:T(8,128)S(1)}, f32[1,8,64]{2,1,0:T(8,128)S(1)}, u32[]{:S(2)}, u32[]{:S(2)}) collective-permute-start(f32[1,8,64]{2,1,0:T(8,128)S(1)} %get-tuple-element.135), channel_id=1, source_target_pairs={{16,0},{17,1},{18,2},{19,3},{20,4},{21,5},{22,6},{23,7},{24,8},{25... | collective-permute-start | bytes 6152 | tf_op jit(solution)/shard_map/ppermute | solution.py:20
  220.6 5.0 %collective-permute-start.45 = (f32[8,1,64]{2,1,0:T(1,128)S(1)}, f32[8,1,64]{2,1,0:T(1,128)S(1)}, u32[]{:S(2)}, u32[]{:S(2)}) collective-permute-start(f32[8,1,64]{2,1,0:T(1,128)S(1)} %get-tuple-element.127), channel_id=1, source_target_pairs={{4,0},{8,4},{12,8},{5,1},{9,5},{13,9},{6,2},{10,6},{14,10},{7,3},{... | collective-permute-start | bytes 6152 | tf_op jit(solution)/shard_map/ppermute | solution.py:20
  225.7 3.6 collective-permute-start.46
  227.6 5.9 %collective-permute-start.47 = (f32[8,10,1]{2,0,1:T(8,128)S(1)}, f32[8,10,1]{2,0,1:T(8,128)S(1)}, u32[]{:S(2)}, u32[]{:S(2)}) collective-permute-start(f32[8,10,1]{2,0,1:T(8,128)S(1)} %get-tuple-element.113), channel_id=1, source_target_pairs={{1,0},{2,1},{3,2},{5,4},{6,5},{7,6},{9,8},{10,9},{11,10},{13,12},{... | collective-permute-start | bytes 968 | tf_op jit(solution)/shard_map/ppermute | solution.py:20
  234.7 5.9 %collective-permute-start.49 = (f32[3,3,4,32]{3,2,1,0:T(4,128)S(1)}, f32[3,3,4,32]{3,2,1,0:T(4,128)S(1)}, u32[]{:S(2)}, u32[]{:S(2)}) collective-permute-start(f32[3,3,4,32]{3,2,1,0:T(4,128)S(1)} %pad_maximum_fusion.36), channel_id=1, source_target_pairs={{16,0},{17,1},{18,2},{19,3},{20,4},{21,5},{22,6},{23,7},{24,8},{25... | collective-permute-start | bytes 13832 | tf_op jit(solution)/shard_map/ppermute | solution.py:20
  236.0 6.0 %collective-permute-start.48 = (f32[3,3,4,32]{3,2,1,0:T(4,128)S(1)}, f32[3,3,4,32]{3,2,1,0:T(4,128)S(1)}, u32[]{:S(2)}, u32[]{:S(2)}) collective-permute-start(f32[3,3,4,32]{3,2,1,0:T(4,128)S(1)} %pad_maximum_fusion.36), channel_id=1, source_target_pairs={{0,16},{1,17},{2,18},{3,19},{4,20},{5,21},{6,22},{7,23},{8,24},{9,... | collective-permute-start | bytes 13832 | tf_op jit(solution)/shard_map/ppermute | solution.py:17
  242.1 3.0 collective-permute-start.50
  243.8 5.2 %collective-permute-start.51 = (f32[3,9,3,32]{3,2,1,0:T(4,128)S(1)}, f32[3,9,3,32]{3,2,1,0:T(4,128)S(1)}, u32[]{:S(2)}, u32[]{:S(2)}) collective-permute-start(f32[3,9,3,32]{3,2,1,0:T(4,128)S(1)} %get-tuple-element.101), channel_id=1, source_target_pairs={{4,0},{8,4},{12,8},{5,1},{9,5},{13,9},{6,2},{10,6},{14,10},{7,3},{... | collective-permute-start | bytes 31112 | tf_op jit(solution)/shard_map/ppermute | solution.py:20
  249.2 5.9 %collective-permute-start.52 = (f32[3,9,10,3]{3,2,1,0:T(8,128)S(1)}, f32[3,9,10,3]{3,2,1,0:T(8,128)S(1)}, u32[]{:S(2)}, u32[]{:S(2)}) collective-permute-start(f32[3,9,10,3]{3,2,1,0:T(8,128)S(1)} %get-tuple-element.53), channel_id=1, source_target_pairs={{0,1},{1,2},{2,3},{4,5},{5,6},{6,7},{8,9},{9,10},{10,11},{12,13},{... | collective-permute-start | bytes 9728 | tf_op jit(solution)/shard_map/ppermute | solution.py:17
  251.2 8.6 %collective-permute-start.53 = (f32[3,9,10,3]{3,2,1,0:T(8,128)S(1)}, f32[3,9,10,3]{3,2,1,0:T(8,128)S(1)}, u32[]{:S(2)}, u32[]{:S(2)}) collective-permute-start(f32[3,9,10,3]{3,2,1,0:T(8,128)S(1)} %get-tuple-element.54), channel_id=1, source_target_pairs={{1,0},{2,1},{3,2},{5,4},{6,5},{7,6},{9,8},{10,9},{11,10},{13,12},{... | collective-permute-start | bytes 9728 | tf_op jit(solution)/shard_map/ppermute | solution.py:20
  261.3 5.5 %collective-permute-start.54 = (f32[1,8,64]{2,1,0:T(8,128)S(1)}, f32[1,8,64]{2,1,0:T(8,128)S(1)}, u32[]{:S(2)}, u32[]{:S(2)}) collective-permute-start(f32[1,8,64]{2,1,0:T(8,128)S(1)} %get-tuple-element.132), channel_id=1, source_target_pairs={{0,16},{1,17},{2,18},{3,19},{4,20},{5,21},{6,22},{7,23},{8,24},{9,... | collective-permute-start | bytes 6152 | tf_op jit(solution)/shard_map/ppermute | solution.py:17
  265.6 5.5 %collective-permute-start.55 = (f32[1,8,64]{2,1,0:T(8,128)S(1)}, f32[1,8,64]{2,1,0:T(8,128)S(1)}, u32[]{:S(2)}, u32[]{:S(2)}) collective-permute-start(f32[1,8,64]{2,1,0:T(8,128)S(1)} %get-tuple-element.133), channel_id=1, source_target_pairs={{16,0},{17,1},{18,2},{19,3},{20,4},{21,5},{22,6},{23,7},{24,8},{25... | collective-permute-start | bytes 6152 | tf_op jit(solution)/shard_map/ppermute | solution.py:20
  271.1 3.3 collective-permute-start.56
  273.1 4.5 %collective-permute-start.57 = (f32[8,1,64]{2,1,0:T(1,128)S(1)}, f32[8,1,64]{2,1,0:T(1,128)S(1)}, u32[]{:S(2)}, u32[]{:S(2)}) collective-permute-start(f32[8,1,64]{2,1,0:T(1,128)S(1)} %get-tuple-element.125), channel_id=1, source_target_pairs={{4,0},{8,4},{12,8},{5,1},{9,5},{13,9},{6,2},{10,6},{14,10},{7,3},{... | collective-permute-start | bytes 6152 | tf_op jit(solution)/shard_map/ppermute | solution.py:20
  277.7 3.6 collective-permute-start.58
  279.6 5.9 %collective-permute-start.59 = (f32[8,10,1]{2,0,1:T(8,128)S(1)}, f32[8,10,1]{2,0,1:T(8,128)S(1)}, u32[]{:S(2)}, u32[]{:S(2)}) collective-permute-start(f32[8,10,1]{2,0,1:T(8,128)S(1)} %get-tuple-element.108), channel_id=1, source_target_pairs={{1,0},{2,1},{3,2},{5,4},{6,5},{7,6},{9,8},{10,9},{11,10},{13,12},{... | collective-permute-start | bytes 968 | tf_op jit(solution)/shard_map/ppermute | solution.py:20
  287.1 3.0 collective-permute-start.60
  288.8 5.5 %collective-permute-start.61 = (f32[1,16,128]{2,1,0:T(8,128)S(1)}, f32[1,16,128]{2,1,0:T(8,128)S(1)}, u32[]{:S(2)}, u32[]{:S(2)}) collective-permute-start(f32[1,16,128]{2,1,0:T(8,128)S(1)} %get-tuple-element.90), channel_id=1, source_target_pairs={{16,0},{17,1},{18,2},{19,3},{20,4},{21,5},{22,6},{23,7},{24,8},{25... | collective-permute-start | bytes 24584 | tf_op jit(solution)/shard_map/ppermute | solution.py:20
  295.8 5.5 %collective-permute-start.63 = (f32[14,1,128]{2,1,0:T(1,128)S(1)}, f32[14,1,128]{2,1,0:T(1,128)S(1)}, u32[]{:S(2)}, u32[]{:S(2)}) collective-permute-start(f32[14,1,128]{2,1,0:T(1,128)S(1)} %get-tuple-element.74), channel_id=1, source_target_pairs={{4,0},{8,4},{12,8},{5,1},{9,5},{13,9},{6,2},{10,6},{14,10},{7,3},{... | collective-permute-start | bytes 21512 | tf_op jit(solution)/shard_map/ppermute | solution.py:20
  301.3 45.6 %collective-permute-start.64 = (f32[14,18,1]{2,0,1:T(8,128)S(1)}, f32[14,18,1]{2,0,1:T(8,128)S(1)}, u32[]{:S(2)}, u32[]{:S(2)}) collective-permute-start(f32[14,18,1]{2,0,1:T(8,128)S(1)} %get-tuple-element.62), channel_id=1, source_target_pairs={{0,1},{1,2},{2,3},{4,5},{5,6},{6,7},{8,9},{9,10},{10,11},{12,13},{... | collective-permute-start | bytes 3032 | tf_op jit(solution)/shard_map/ppermute | solution.py:17
  303.3 43.7 %collective-permute-start.65 = (f32[14,18,1]{2,0,1:T(8,128)S(1)}, f32[14,18,1]{2,0,1:T(8,128)S(1)}, u32[]{:S(2)}, u32[]{:S(2)}) collective-permute-start(f32[14,18,1]{2,0,1:T(8,128)S(1)} %get-tuple-element.63), channel_id=1, source_target_pairs={{1,0},{2,1},{3,2},{5,4},{6,5},{7,6},{9,8},{10,9},{11,10},{13,12},{... | collective-permute-start | bytes 3032 | tf_op jit(solution)/shard_map/ppermute | solution.py:20
  348.5 5.5 %collective-permute-start.66 = (f32[1,16,128]{2,1,0:T(8,128)S(1)}, f32[1,16,128]{2,1,0:T(8,128)S(1)}, u32[]{:S(2)}, u32[]{:S(2)}) collective-permute-start(f32[1,16,128]{2,1,0:T(8,128)S(1)} %get-tuple-element.86), channel_id=1, source_target_pairs={{0,16},{1,17},{2,18},{3,19},{4,20},{5,21},{6,22},{7,23},{8,24},{9,... | collective-permute-start | bytes 24584 | tf_op jit(solution)/shard_map/ppermute | solution.py:17
  352.6 5.5 %collective-permute-start.67 = (f32[1,16,128]{2,1,0:T(8,128)S(1)}, f32[1,16,128]{2,1,0:T(8,128)S(1)}, u32[]{:S(2)}, u32[]{:S(2)}) collective-permute-start(f32[1,16,128]{2,1,0:T(8,128)S(1)} %get-tuple-element.87), channel_id=1, source_target_pairs={{16,0},{17,1},{18,2},{19,3},{20,4},{21,5},{22,6},{23,7},{24,8},{25... | collective-permute-start | bytes 24584 | tf_op jit(solution)/shard_map/ppermute | solution.py:20
  359.5 5.4 %collective-permute-start.69 = (f32[14,1,128]{2,1,0:T(1,128)S(1)}, f32[14,1,128]{2,1,0:T(1,128)S(1)}, u32[]{:S(2)}, u32[]{:S(2)}) collective-permute-start(f32[14,1,128]{2,1,0:T(1,128)S(1)} %get-tuple-element.72), channel_id=1, source_target_pairs={{4,0},{8,4},{12,8},{5,1},{9,5},{13,9},{6,2},{10,6},{14,10},{7,3},{... | collective-permute-start | bytes 21512 | tf_op jit(solution)/shard_map/ppermute | solution.py:20
  365.0 4.6 %collective-permute-start.70 = (f32[14,18,1]{2,0,1:T(8,128)S(1)}, f32[14,18,1]{2,0,1:T(8,128)S(1)}, u32[]{:S(2)}, u32[]{:S(2)}) collective-permute-start(f32[14,18,1]{2,0,1:T(8,128)S(1)} %get-tuple-element.60), channel_id=1, source_target_pairs={{0,1},{1,2},{2,3},{4,5},{5,6},{6,7},{8,9},{9,10},{10,11},{12,13},{... | collective-permute-start | bytes 3032 | tf_op jit(solution)/shard_map/ppermute | solution.py:17
  366.8 7.5 %collective-permute-start.71 = (f32[14,18,1]{2,0,1:T(8,128)S(1)}, f32[14,18,1]{2,0,1:T(8,128)S(1)}, u32[]{:S(2)}, u32[]{:S(2)}) collective-permute-start(f32[14,18,1]{2,0,1:T(8,128)S(1)} %get-tuple-element.61), channel_id=1, source_target_pairs={{1,0},{2,1},{3,2},{5,4},{6,5},{7,6},{9,8},{10,9},{11,10},{13,12},{... | collective-permute-start | bytes 3032 | tf_op jit(solution)/shard_map/ppermute | solution.py:20
  (10 other events, 30.0 us)
where the time goes:
time: 378 us; the launch traced here: 376 us
  waiting for transfers between devices  147 us (39%)
  starting transfers between devices  133 us (35%)
  blocking collectives  41.1 us (11%)
  local copies, waits for them, and re-layouts  30 us (8%)
  other arithmetic  21 us (6%)
  between operations  3.85 us (1%)
    ppermute x36, waiting for transfers between devices, with_halo(): lax.ppermute(lax.slice_in_dim(block, 0, width, axis=dim), axis, backward)  131 us
    ppermute x36, starting transfers between devices, with_halo(): lax.ppermute(lax.slice_in_dim(block, block.shape[dim] - width, None, axis...  86.4 us
    ppermute x36, starting transfers between devices, with_halo(): lax.ppermute(lax.slice_in_dim(block, 0, width, axis=dim), axis, backward)  46.7 us
    psum x1, blocking collectives, shards(): lax.psum((jnp.sum(residual * precond), jnp.sum(image * precond)), ('gx',...  41.1 us
    reshape x5, local copies, waits for them, and re-layouts, restrict(): values.reshape(extent[0] // 2, 2, extent[1] // 2, 2, extent[2] // 2, 2)  25.2 us
    ppermute x36, waiting for transfers between devices, with_halo(): lax.ppermute(lax.slice_in_dim(block, block.shape[dim] - width, None, axis...  15.8 us
    reduce_sum x6, other arithmetic, restrict(): return 0.5 * grouped.sum(axis=(1, 3, 5))  10.3 us
  transfers between devices with their start and end apart: 72, of which 44 were waited for; matrix products, arithmetic and copies ran while one was open for 3% of the time, Pallas kernels for 0%

commit v1 on v0

v1 whole, which is shorter than its diff:
```python
import functools

import jax
import jax.numpy as jnp
from jax import lax
from jax.experimental import pallas as pl
from jax.experimental.pallas import tpu as pltpu
from jax.sharding import PartitionSpec as P

SWEEPS = 4
relaxation = 0.6

AXES = ("gx", "gy", "gz")
MESH = pl.DeviceIdType.MESH
WIDTH = 5
EDGE = 8
SPAN = 2 * WIDTH
PART = SWEEPS


def dot(a, b):
    return jnp.dot(a, b, preferred_element_type=jnp.float32, precision=lax.Precision.HIGHEST)


def iota(shape, dim):
    return lax.broadcasted_iota(jnp.int32, shape, dim)


def kernel(counts, block, reach, g_ref, c_ref, sol_ref, res_ref, pre_ref, img_ref,
           gc0, im0, pk1, pk2, zr1, zr2, t1, d0, d1, xr0, xr1, pf0, pf1, xm, um,
           cs1, cs2, cr1, cr2, mid, red_s, red_r, ssem, rsem, lssem, lrsem):
    bx, by, bz = block
    kx = reach
    me = [lax.axis_index(a) for a in AXES]
    ex, ey = bx + SPAN, by + 2 * EDGE
    mx, my = bx // 2 + 4, ey // 2
    qx = bx // 4
    lane = iota((ey, bz), 1)
    row = iota((ey, bz), 0)

    def valid(offset):
        ok = None
        for axis, step in enumerate(offset):
            if step == 0:
                continue
            place = me[axis] + step
            term = place >= 0 if step < 0 else place < counts[axis]
            ok = term if ok is None else jnp.logical_and(ok, term)
        return ok

    def target(offset):
        return tuple(m + s for m, s in zip(me, offset))

    near = [(dx, dy, dz) for dx in range(-kx, kx + 1) for dy in (-1, 0, 1) for dz in (-1, 0, 1)]
    near = [o for o in near if o != (0, 0, 0) and all(counts[a] > abs(o[a]) for a in range(3))]
    close = [o for o in near if abs(o[0]) <= 1]

    barrier = pltpu.get_barrier_semaphore()
    lines = []
    for axis in range(3):
        for step in range(1, counts[axis]):
            to = list(me)
            to[axis] = lax.rem(me[axis] + step, counts[axis])
            lines.append((axis, step, tuple(to)))

    zr1[...] = jnp.zeros_like(zr1)
    zr2[...] = jnp.zeros_like(zr2)
    gc0[...] = jnp.zeros_like(gc0)
    im0[...] = jnp.zeros_like(im0)
    cr1[...] = jnp.zeros_like(cr1)
    cr2[...] = jnp.zeros_like(cr2)

    for offset in near:
        @pl.when(valid(offset))
        def _(offset=offset):
            pl.semaphore_signal(barrier, inc=1, device_id=target(offset), device_id_type=MESH)
    for axis, step, to in lines:
        pl.semaphore_signal(barrier, inc=1, device_id=to, device_id_type=MESH)

    def options(axis, far):
        total = 1
        for step in range(1, far + 1):
            if counts[axis] > step:
                total = total + (me[axis] >= step).astype(jnp.int32)
                total = total + (me[axis] + step < counts[axis]).astype(jnp.int32)
        return total

    greeted = options(0, kx) * options(1, 1) * options(2, 1) - 1 + len(lines)

    strip = (lane[:by] < WIDTH) | (lane[:by] >= bz - WIDTH)

    def packed(planes):
        total = None
        for i, plane in enumerate(planes):
            piece = jnp.where(strip, plane, 0.0)
            if i > 0:
                piece = pltpu.roll(piece, SPAN * i, 1)
            total = piece if total is None else total + piece
        return total

    def fill(buf, pk, s, planes):
        for i, plane in enumerate(planes):
            buf[s, WIDTH + i, EDGE:EDGE + by, :] = plane
        pk[s] = packed(planes)

    def row_ends(dy):
        if dy == 0:
            return 0, by, EDGE
        if dy > 0:
            return by - EDGE, EDGE, 0
        return 0, EDGE, EDGE + by

    def fine_copy(phase, n, offset, buf, pk, zr):
        dx, dy, dz = offset
        start, size, goes = row_ends(dy)
        if dz == 0:
            if dx == 0:
                px, nx, tx = WIDTH, bx, WIDTH
            elif dx > 0:
                px, nx, tx = bx, WIDTH, 0
            else:
                px, nx, tx = WIDTH, WIDTH, WIDTH + bx
            src = buf.at[:, pl.ds(px, nx), pl.ds(EDGE + start, size), :]
            dst = buf.at[:, pl.ds(tx, nx), pl.ds(goes, size), :]
        else:
            side = 0 if dz > 0 else 1
            src = pk.at[:, pl.ds(start, size), :]
            dst = zr.at[side, 1 - dx, :, pl.ds(goes, size), :]
        return pltpu.make_async_remote_copy(
            src_ref=src, dst_ref=dst, send_sem=ssem.at[phase, n], recv_sem=rsem.at[phase, n],
            device_id=target(offset), device_id_type=MESH)

    def coarse_copy(phase, n, offset, cs, cr):
        dx, dy, dz = offset
        return pltpu.make_async_remote_copy(
            src_ref=cs, dst_ref=cr.at[kx - dx, 1 - dy, 1 - dz],
            send_sem=ssem.at[phase, n], recv_sem=rsem.at[phase, n],
            device_id=target(offset), device_id_type=MESH)

    def begin(make, offsets):
        for n, offset in enumerate(offsets):
            @pl.when(valid(offset))
            def _(n=n, offset=offset):
                make(n, offset).start()

    def arrive(make, offsets):
        for n, offset in enumerate(offsets):
            @pl.when(valid(tuple(-s for s in offset)))
            def _(n=n, offset=offset):
                make(n, offset).wait_recv()

    def leave(make, offsets):
        for n, offset in enumerate(offsets):
            @pl.when(valid(offset))
            def _(n=n, offset=offset):
                make(n, offset).wait_send()

    def line_copy(axis, step, to):
        n = sum(counts[:axis]) + step
        return pltpu.make_async_remote_copy(
            src_ref=red_s.at[axis], dst_ref=red_r.at[n], send_sem=lssem.at[n],
            recv_sem=lrsem.at[n], device_id=to, device_id_type=MESH)

    def line_begin(axis, value):
        red_s[axis] = value
        for a, step, to in lines:
            if a == axis:
                line_copy(a, step, to).start()

    def line_end(axis):
        value = red_s[axis]
        for a, step, to in lines:
            if a == axis:
                line_copy(a, step, to).wait_recv()
                value = value + red_r[sum(counts[:a]) + step]
        return value

    place = lax.rem(lane + WIDTH, bz)
    low = lax.rem(place, SPAN) < WIDTH
    band = (lane < WIDTH) | (lane >= bz - WIDTH)

    def spread(zr, s, t):
        for side in range(3):
            merged = jnp.where(low, zr[0, side, s], zr[1, side, s])
            if side == 0:
                todo = [(bx - WIDTH + i, i) for i in range(WIDTH)]
            elif side == 1:
                todo = [(i, WIDTH + i) for i in range(bx)]
            else:
                todo = [(i, WIDTH + bx + i) for i in range(WIDTH)]
            for i, e in todo:
                piece = merged if i == 0 else pltpu.roll(merged, (bz - SPAN * i) % bz, 1)
                t1[t, e] = jnp.where(band, piece, 0.0)

    first, last = lane == 0, lane == bz - 1

    def yz(a, b):
        sa = a + jnp.where(first, pltpu.roll(b, 1, 1), pltpu.roll(a, 1, 1))
        sb = b + jnp.where(first, pltpu.roll(a, 1, 1), pltpu.roll(b, 1, 1))
        sa = sa + jnp.where(last, pltpu.roll(b, bz - 1, 1), pltpu.roll(a, bz - 1, 1))
        sb = sb + jnp.where(last, pltpu.roll(a, bz - 1, 1), pltpu.roll(b, bz - 1, 1))
        sa = sa + pltpu.roll(sa, 1, 0) + pltpu.roll(sa, ey - 1, 0)
        sb = sb + pltpu.roll(sb, 1, 0) + pltpu.roll(sb, ey - 1, 0)
        return sa, sb

    def box(v):
        s = v + pltpu.roll(v, 1, 2) + pltpu.roll(v, v.shape[2] - 1, 2)
        s = s + pltpu.roll(s, 1, 1) + pltpu.roll(s, v.shape[1] - 1, 1)
        zero = jnp.zeros_like(s[:1])
        return s + jnp.concatenate([zero, s[:-1]], 0) + jnp.concatenate([s[1:], zero], 0)

    p_, q_ = iota((bz, bz), 0), iota((bz, bz), 1)
    down_a = jnp.where((p_ >> 1) == q_, 0.5, 0.0)
    down_b = jnp.where(((p_ + bz) >> 1) == q_, 0.5, 0.0)
    up_a = jnp.where((q_ >> 1) == p_, 1.0, 0.0)
    up_b = jnp.where(((q_ + bz) >> 1) == p_, 1.0, 0.0)
    quarter = bz // 4
    down_c = jnp.where((p_ < bz // 2) & ((p_ >> 1) == lax.rem(q_, quarter)), 0.5, 0.0)
    up_c = jnp.where(p_ == jnp.where(q_ < 3 * quarter, q_ >> 1, (q_ >> 1) + bz // 2), 1.0, 0.0)

    def restricted(of):
        for m in range(mx):
            a0, b0 = of(2 * m + 1)
            a1, b1 = of(2 * m + 2)
            xr0[m * ey:(m + 1) * ey, :] = a0 + a1
            xr1[m * ey:(m + 1) * ey, :] = b0 + b1
        n = mx * my
        a = xr0[pl.ds(0, n, stride=2), :] + xr0[pl.ds(1, n, stride=2), :]
        b = xr1[pl.ds(0, n, stride=2), :] + xr1[pl.ds(1, n, stride=2), :]
        return (dot(a, down_a) + dot(b, down_b)).reshape(mx, my, bz)

    def coarsened(v):
        for m in range(qx):
            xm[m * my:(m + 1) * my, :] = v[2 + 2 * m] + v[3 + 2 * m]
        n = qx * my // 2
        a = xm[pl.ds(0, n, stride=2), :] + xm[pl.ds(1, n, stride=2), :]
        a = dot(a, down_c).reshape(qx, my // 2, bz)
        upper = iota(a.shape, 1) < my // 4
        return jnp.where(upper, pltpu.roll(a, my // 2 - 2, 1), pltpu.roll(a, 2, 1))

    clane = iota((my // 2, bz), 1)
    crow = iota((my // 2, bz), 0)
    xs = [x for x in range(-PART, qx + PART) if -kx * qx <= x < (kx + 1) * qx]

    def gathered(cr, cs, s):
        def tile(dx, dy, x):
            def piece(dz):
                if (dx, dy, dz) == (0, 0, 0):
                    return cs[s, x]
                return cr[kx + dx, 1 + dy, 1 + dz, s, x]
            v = jnp.where(clane >= 3 * quarter, piece(-1), piece(0))
            return jnp.where((clane >= quarter) & (clane < 2 * quarter), piece(1), v)

        planes = []
        for x in xs:
            dx = x // qx
            i = x - dx * qx
            upper = jnp.where(crow < my // 4, tile(dx, -1, i), tile(dx, 0, i))
            lower = jnp.where(crow < my // 4, tile(dx, 1, i), 0.0)
            planes.append(jnp.concatenate([upper, lower], 0))
        return jnp.stack(planes)

    def within(place, axis, size):
        place = place + me[axis] * size
        return (place >= 0) & (place < counts[axis] * size)

    g = [g_ref[i] for i in range(bx)]
    fill(gc0, pk1, 0, g)
    fill(gc0, pk1, 1, [c_ref[i] for i in range(bx)])
    pl.semaphore_wait(barrier, greeted)
    make_a = lambda n, o: fine_copy(0, n, o, gc0, pk1, zr1)
    begin(make_a, close)
    arrive(make_a, close)
    spread(zr1, 0, 0)
    spread(zr1, 1, 1)

    in_y = within(row - EDGE, 1, by)
    in_z = band & within(jnp.where(lane < bz // 2, lane + bz, lane - bz), 2, bz)
    for i in range(ex):
        in_x = within(jnp.full((ey, bz), i - WIDTH, jnp.int32), 0, bx)
        d0[i] = jnp.where(in_y & in_x, relaxation / (26.0 + gc0[1, i]), 0.0)
        d1[i] = jnp.where(in_y & in_x & in_z, relaxation / (26.0 + t1[1, i]), 0.0)

    c1 = restricted(lambda i: (gc0[1, i], t1[1, i]))
    shape = (mx, my, bz)
    zl = iota(shape, 2)
    zl = jnp.where(zl < 3 * quarter, zl, zl - bz)
    inside = within(iota(shape, 0) - 2, 0, bx // 2) & within(iota(shape, 1) - 4, 1, by // 2)
    inside = inside & within(zl, 2, bz // 2)
    mid[0] = jnp.where(inside, relaxation / (26.0 + c1), 0.0)
    mid[1] = 27.0 + c1
    cs1[1] = coarsened(c1)

    def inverse2(c2):
        shape = c2.shape
        z = iota(shape, 2)
        z = jnp.where(z < 2 * quarter, z, z - bz)
        ok = within(iota(shape, 0) + xs[0], 0, qx) & within(iota(shape, 1) - 4, 1, by // 4)
        ok = ok & within(z, 2, quarter) & (z >= -quarter)
        return jnp.where(ok, relaxation / (26.0 + c2), 0.0)

    def cycle(g_at, make_b, cs, cr, hook, second, finish):
        def e0(i):
            a, b = g_at(i)
            return d0[i] * a, d1[i] * b

        sums = {}

        def remainder(i):
            for k in (i - 1, i, i + 1):
                if k not in sums:
                    sums[k] = yz(*e0(k))
            a, b = g_at(i)
            ea, eb = e0(i)
            ra = a - (27.0 + gc0[1, i]) * ea + sums[i - 1][0] + sums[i][0] + sums[i + 1][0]
            rb = b - (27.0 + t1[1, i]) * eb + sums[i - 1][1] + sums[i][1] + sums[i + 1][1]
            return ra, rb

        g1 = restricted(remainder)
        f = mid[0] * g1
        mid[2] = g1
        cs[0] = coarsened(g1 - mid[1] * f + box(f))
        begin(make_b, near)
        hook()
        arrive(make_b, near)
        g2 = gathered(cr, cs, 0)
        c2 = gathered(cr1, cs1, 1)
        inv = inverse2(c2)
        diag = 27.0 + c2
        e = inv * g2
        for sweep in range(SWEEPS - 1):
            e = e + inv * (g2 - diag * e + box(e))
        second()
        nq = qx + 2
        e = jnp.concatenate([e[xs.index(x)][None] if x in xs else jnp.zeros_like(e[:1])
                             for x in range(-1, qx + 1)], 0)
        e = pltpu.roll(e, my - 2, 1)[:, :my // 2].reshape(nq * my // 2, bz)
        u = dot(e, up_c)
        um[pl.ds(0, nq * my // 2, stride=2), :] = u
        um[pl.ds(1, nq * my // 2, stride=2), :] = u
        u = um[...].reshape(nq, my, bz)
        u = jnp.concatenate([u[(m - 2) // 2 + 1][None] for m in range(mx)], 0)
        g1 = mid[2]
        f = mid[0] * g1 + u
        f = f + mid[0] * (g1 - mid[1] * f + box(f))
        nm = mx - 2
        f = f[1:mx - 1].reshape(nm * my, bz)
        for pf, up in ((pf0, up_a), (pf1, up_b)):
            w = dot(f, up)
            pf[pl.ds(0, nm * my, stride=2), :] = w
            pf[pl.ds(1, nm * my, stride=2), :] = w

        def e1(i):
            m = (i - WIDTH) // 2 + 1
            a, b = e0(i)
            return a + pf0[m * ey:(m + 1) * ey, :], b + pf1[m * ey:(m + 1) * ey, :]

        sums1, sums2 = {}, {}
        e2 = {}
        for i in range(WIDTH - 1, WIDTH + bx + 1):
            for k in (i - 1, i, i + 1):
                if k not in sums1:
                    sums1[k] = yz(*e1(k))
            ga, gb = g_at(i)
            ea, eb = e1(i)
            s = [sums1[i - 1][t] + sums1[i][t] + sums1[i + 1][t] for t in range(2)]
            za = ea + d0[i] * (ga - (27.0 + gc0[1, i]) * ea + s[0])
            zb = eb + d1[i] * (gb - (27.0 + t1[1, i]) * eb + s[1])
            e2[i] = za[EDGE:EDGE + by]
            sums2[i] = yz(za, zb)[0][EDGE:EDGE + by]
            k = i - 1
            if k - 1 in sums2:
                out = (27.0 + c_ref[k - WIDTH]) * e2[k] - (sums2[k - 1] + sums2[k] + sums2[k + 1])
                finish(k - WIDTH, e2[k], out)

    gamma, delta = [], []
    images = []

    def finish1(i, e, out):
        pre_ref[i] = e
        images.append(out)
        gamma.append(g_ref[i] * e)
        delta.append(out * e)

    nothing = lambda: None
    make_b = lambda n, o: coarse_copy(1, n, o, cs1, cr1)
    cycle(lambda i: (gc0[0, i], t1[0, i]), make_b, cs1, cr1, nothing, nothing, finish1)

    for i in range(bx):
        img_ref[i] = images[i]
    fill(im0, pk2, 0, images)
    make_c = lambda n, o: fine_copy(2, n, o, im0, pk2, zr2)
    begin(make_c, close)
    gs = jnp.sum(sum(gamma[1:], gamma[0]), axis=0, keepdims=True)
    ds = jnp.sum(sum(delta[1:], delta[0]), axis=0, keepdims=True)
    line_begin(2, jnp.where(iota((8, bz), 0) == 0, gs, ds))
    arrive(make_c, close)
    spread(zr2, 0, 2)

    state = []

    def hook():
        line_begin(1, line_end(2))

    def second():
        line_begin(0, line_end(1))

    def finish2(i, e, out):
        if not state:
            total = line_end(0)
            total = jnp.sum(total, axis=1, keepdims=True)
            state.append(total[0:1] / total[1:2])
        alpha = state[0]
        p, im = pre_ref[i], img_ref[i]
        sol_ref[i] = alpha * p
        res_ref[i] = g_ref[i] - alpha * im
        pre_ref[i] = p - alpha * e
        img_ref[i] = im - alpha * out

    make_d = lambda n, o: coarse_copy(3, n, o, cs2, cr2)
    cycle(lambda i: (im0[0, i], t1[2, i]), make_d, cs2, cr2, hook, second, finish2)

    leave(make_a, close)
    leave(make_b, near)
    leave(make_c, close)
    leave(make_d, near)
    for axis, step, to in lines:
        line_copy(axis, step, to).wait_send()


def solution(mesh):
    counts = tuple(mesh.shape[a] for a in AXES)

    def shards(right_side, coefficient):
        bx, by, bz = block = right_side.shape
        assert SPAN * bx <= bz and by == 16 and bx % 4 == 0
        kx = max(1, min(-(-PART // (bx // 4)), counts[0] - 1))
        ex, ey = bx + SPAN, by + 2 * EDGE
        mx, my = bx // 2 + 4, ey // 2
        qx = bx // 4
        most = (2 * kx + 1) * 9
        f32 = jnp.float32
        out = jax.ShapeDtypeStruct(block, f32)
        vmem = pl.BlockSpec(memory_space=pltpu.VMEM)
        return tuple(pl.pallas_call(
            functools.partial(kernel, counts, block, kx),
            out_shape=[out] * 4,
            in_specs=[vmem] * 2,
            out_specs=[vmem] * 4,
            scratch_shapes=[
                pltpu.VMEM((2, ex, ey, bz), f32),
                pltpu.VMEM((1, ex, ey, bz), f32),
                pltpu.VMEM((2, by, bz), f32),
                pltpu.VMEM((1, by, bz), f32),
                pltpu.VMEM((2, 3, 2, ey, bz), f32),
                pltpu.VMEM((2, 3, 1, ey, bz), f32),
                pltpu.VMEM((3, ex, ey, bz), f32),
                pltpu.VMEM((ex, ey, bz), f32),
                pltpu.VMEM((ex, ey, bz), f32),
                pltpu.VMEM((mx * ey, bz), f32),
                pltpu.VMEM((mx * ey, bz), f32),
                pltpu.VMEM(((mx - 2) * ey, bz), f32),
                pltpu.VMEM(((mx - 2) * ey, bz), f32),
                pltpu.VMEM((qx * my, bz), f32),
                pltpu.VMEM(((qx + 2) * my, bz), f32),
                pltpu.VMEM((2, qx, my // 2, bz), f32),
                pltpu.VMEM((1, qx, my // 2, bz), f32),
                pltpu.VMEM((2 * kx + 1, 3, 3, 2, qx, my // 2, bz), f32),
                pltpu.VMEM((2 * kx + 1, 3, 3, 1, qx, my // 2, bz), f32),
                pltpu.VMEM((3, mx, my, bz), f32),
                pltpu.VMEM((3, 8, bz), f32),
                pltpu.VMEM((sum(counts), 8, bz), f32),
                pltpu.SemaphoreType.DMA((4, most)),
                pltpu.SemaphoreType.DMA((4, most)),
                pltpu.SemaphoreType.DMA((sum(counts),)),
                pltpu.SemaphoreType.DMA((sum(counts),)),
            ],
            compiler_params=pltpu.CompilerParams(collective_id=0, has_side_effects=True),
            name="relayed",
        )(right_side, coefficient))

    placed = (P(*AXES), P(*AXES))
    return jax.shard_map(
        shards, mesh=mesh, in_specs=placed, out_specs=(P(*AXES),) * 4, check_vma=False
    )
```

time: 378 us -> 41.5 us (0.11)
  waiting for transfers between devices: 147 us -> 0 us
  starting transfers between devices: 133 us -> 0 us
  blocking collectives: 41.1 us -> 0 us
  Pallas kernels: 0 us -> 36.6 us
  local copies, waits for them, and re-layouts: 30 us -> 4.07 us
  other arithmetic: 21 us -> 0 us
    ppermute x72 -> x0, waiting for transfers between devices: 147 us -> none  [the longest x36 131 us: with_halo(): lax.ppermute(lax.slice_in_dim(block, 0, width, axis=dim), axis, backward)]
    ppermute x72 -> x0, starting transfers between devices: 133 us -> none  [the longest x36 86.4 us: with_halo(): lax.ppermute(lax.slice_in_dim(block, block.shape[dim] - width, None, axis...]
    psum x1 -> x0, blocking collectives: 41.1 us -> none  [shards(): lax.psum((jnp.sum(residual * precond), jnp.sum(image * precond)), ('gx',...]
    pallas_call x0 -> x1, Pallas kernels: none -> 36.6 us  [shards(): pl.pallas_call(functools.partial(kernel, counts, block, kx), out_shape=[o...]
    reshape x13 -> x0, local copies, waits for them, and re-layouts: 26.3 us -> none  [the longest x5 25.2 us: restrict(): values.reshape(extent[0] // 2, 2, extent[1] // 2, 2, extent[2] // 2, 2)]
    reduce_sum x7 -> x0, other arithmetic: 10.9 us -> none  [the longest x6 10.3 us: restrict(): return 0.5 * grouped.sum(axis=(1, 3, 5))]
    add x40 -> x0, other arithmetic: 3.98 us -> none  [the longest x16 2.99 us: block_sum(): summed = padded[:-2] + padded[1:-1] + padded[2:]]
    unnamed x16 -> x10, local copies, waits for them, and re-layouts: 0.25 us -> 4.07 us
  transfers between devices with their start and end apart: 72 -> 0, of which waited for: 44 -> 0; matrix products, arithmetic and copies ran while one was open for 3% -> 0% of each run, Pallas kernels for 0% -> 0%
where the time goes in v1:
time: 41.5 us; the launch traced here: 41.3 us
  Pallas kernels  36.6 us (88%)
  local copies, waits for them, and re-layouts  4.07 us (10%)
  between operations  0.65 us (2%)
    pallas_call x1, Pallas kernels, shards(): pl.pallas_call(functools.partial(kernel, counts, block, kx), out_shape=[o...  36.6 us
    unnamed x10, local copies, waits for them, and re-layouts  4.07 us

profile of v1, /device:TPU:0, one launch (start us, length us, event | category | flops | bytes accessed | tf_op | source)
XLA Modules:
  0.0 41.3 jit_solution(12973213111357015733)
XLA Ops:
  0.6 36.6 %relayed.1 = (f32[12,16,128]{2,1,0:T(8,128)}, f32[12,16,128]{2,1,0:T(8,128)}, f32[12,16,128]{2,1,0:T(8,128)}, f32[12,16,128]{2,1,0:T(8,128)}) custom-call(f32[12,16,128]{2,1,0:T(8,128)} %g_ref.1, f32[12,16,128]{2,1,0:T(8,128)} %c_ref.1), custom_call_target="tpu_custom_call" | custom-call | tf_op jit(solution)/shard_map/relayed/pallas_call | solution.py:445
  37.2 0.0 copy-start.2
  37.2 1.6 %copy.10 = f32[12,16,128]{2,1,0:T(8,128)} copy(f32[12,16,128]{2,1,0:T(8,128)} %get-tuple-element.8) | data formatting | bytes 196608
  38.8 0.0 copy-done.2
  38.8 0.0 copy-start.1
  38.8 0.6 %copy.11 = f32[12,16,128]{2,1,0:T(8,128)} copy(f32[12,16,128]{2,1,0:T(8,128)S(1)} %copy-done.2) | data formatting | bytes 196608
  39.4 0.3 copy-done.1
  39.7 0.0 copy-start
  39.7 0.6 %copy.12 = f32[12,16,128]{2,1,0:T(8,128)} copy(f32[12,16,128]{2,1,0:T(8,128)S(1)} %copy-done.1) | data formatting | bytes 196608
  40.4 0.3 copy-done
  40.7 0.6 %copy.13 = f32[12,16,128]{2,1,0:T(8,128)} copy(f32[12,16,128]{2,1,0:T(8,128)S(1)} %copy-done) | data formatting | bytes 196608
Async XLA Ops:
  37.2 1.6 %copy-start.2 = (f32[12,16,128]{2,1,0:T(8,128)S(1)}, f32[12,16,128]{2,1,0:T(8,128)}, u32[]{:S(2)}) copy-start(f32[12,16,128]{2,1,0:T(8,128)} %get-tuple-element.9) | copy-start | bytes 294916
  38.8 0.9 %copy-start.1 = (f32[12,16,128]{2,1,0:T(8,128)S(1)}, f32[12,16,128]{2,1,0:T(8,128)}, u32[]{:S(2)}) copy-start(f32[12,16,128]{2,1,0:T(8,128)} %get-tuple-element.10) | copy-start | bytes 294916
  39.7 0.9 %copy-start = (f32[12,16,128]{2,1,0:T(8,128)S(1)}, f32[12,16,128]{2,1,0:T(8,128)}, u32[]{:S(2)}) copy-start(f32[12,16,128]{2,1,0:T(8,128)} %get-tuple-element.11) | copy-start | bytes 294916

commit v2 on v1

--- a/solution.py
+++ b/solution.py
@@ -19,16 +19,20 @@
 
 
 def dot(a, b):
-    return jnp.dot(a, b, preferred_element_type=jnp.float32, precision=lax.Precision.HIGHEST)
+    high = a.astype(jnp.bfloat16)
+    low = (a - high.astype(jnp.float32)).astype(jnp.bfloat16)
+    both = jnp.concatenate([high, low], 1)
+    b = b.astype(jnp.bfloat16)
+    return jnp.dot(both, jnp.concatenate([b, b], 0), preferred_element_type=jnp.float32)
 
 
 def iota(shape, dim):
     return lax.broadcasted_iota(jnp.int32, shape, dim)
 
 
-def kernel(counts, block, reach, g_ref, c_ref, sol_ref, res_ref, pre_ref, img_ref,
+def kernel(counts, block, reach, g_ref, c_ref, pre_ref, img_ref, twice_ref, image_twice_ref, alpha_ref,
            gc0, im0, pk1, pk2, zr1, zr2, t1, d0, d1, xr0, xr1, pf0, pf1, xm, um,
-           cs1, cs2, cr1, cr2, mid, red_s, red_r, ssem, rsem, lssem, lrsem):
+           cs1, cs2, cr1, cr2, kept, mid, red_s, red_r, ssem, rsem, lssem, lrsem):
     bx, by, bz = block
     kx = reach
     me = [lax.axis_index(a) for a in AXES]
@@ -53,6 +57,7 @@
 
     near = [(dx, dy, dz) for dx in range(-kx, kx + 1) for dy in (-1, 0, 1) for dz in (-1, 0, 1)]
     near = [o for o in near if o != (0, 0, 0) and all(counts[a] > abs(o[a]) for a in range(3))]
+    near.sort(key=lambda o: (-abs(o[0]), abs(o[1]) + abs(o[2])))
     close = [o for o in near if abs(o[0]) <= 1]
 
     barrier = pltpu.get_barrier_semaphore()
@@ -229,36 +234,50 @@
         b = xr1[pl.ds(0, n, stride=2), :] + xr1[pl.ds(1, n, stride=2), :]
         return (dot(a, down_a) + dot(b, down_b)).reshape(mx, my, bz)
 
-    def coarsened(v):
+    turn = iota((my // 2, bz), 1) // quarter
+    crow = iota((my // 2, bz), 0)
+
+    def coarsened(v, lift):
         for m in range(qx):
             xm[m * my:(m + 1) * my, :] = v[2 + 2 * m] + v[3 + 2 * m]
         n = qx * my // 2
         a = xm[pl.ds(0, n, stride=2), :] + xm[pl.ds(1, n, stride=2), :]
-        a = dot(a, down_c).reshape(qx, my // 2, bz)
-        upper = iota(a.shape, 1) < my // 4
-        return jnp.where(upper, pltpu.roll(a, my // 2 - 2, 1), pltpu.roll(a, 2, 1))
-
-    clane = iota((my // 2, bz), 1)
-    crow = iota((my // 2, bz), 0)
+        a = dot(a, down_c)
+        rows = my // 2
+        tile = a[:rows]
+        for m in range(1, qx):
+            tile = jnp.where(turn == m, a[m * rows:(m + 1) * rows], tile)
+        return pltpu.roll(tile, 2 if lift else rows - 2, 0)
+
     xs = [x for x in range(-PART, qx + PART) if -kx * qx <= x < (kx + 1) * qx]
 
-    def gathered(cr, cs, s):
-        def tile(dx, dy, x):
-            def piece(dz):
-                if (dx, dy, dz) == (0, 0, 0):
-                    return cs[s, x]
-                return cr[kx + dx, 1 + dy, 1 + dz, s, x]
-            v = jnp.where(clane >= 3 * quarter, piece(-1), piece(0))
-            return jnp.where((clane >= quarter) & (clane < 2 * quarter), piece(1), v)
-
-        planes = []
-        for x in xs:
-            dx = x // qx
-            i = x - dx * qx
-            upper = jnp.where(crow < my // 4, tile(dx, -1, i), tile(dx, 0, i))
-            lower = jnp.where(crow < my // 4, tile(dx, 1, i), 0.0)
-            planes.append(jnp.concatenate([upper, lower], 0))
-        return jnp.stack(planes)
+    def gathered(cr, cs, lifts):
+        half = my // 4
+        columns = {}
+        for dx in sorted({x // qx for x in xs}):
+            for dy in (-1, 0, 1):
+                here = cs[...] if (dx, dy) == (0, 0) else cr[kx + dx, 1 + dy, 1]
+                after = pltpu.roll(cr[kx + dx, 1 + dy, 2], quarter, 1)
+                before = pltpu.roll(cr[kx + dx, 1 + dy, 0], 3 * quarter, 1)
+                for m in range(qx):
+                    tile = jnp.where(turn == (m + 1) % 4, after, here)
+                    tile = jnp.where(turn == (m + 3) % 4, before, tile)
+                    if m > 0:
+                        tile = pltpu.roll(tile, bz - quarter * m, 1)
+                    columns[dx * qx + m, dy] = tile
+        arrays = []
+        for lift in lifts:
+            planes = []
+            for x in xs:
+                tiles = [columns[x, dy] for dy in (-1, 0, 1)]
+                turned = [pltpu.roll(t, half, 0) for t in tiles]
+                if lift:
+                    tiles, turned = turned, tiles
+                upper = jnp.where(crow < half, tiles[0], turned[1])
+                lower = jnp.where(crow < half, tiles[2], 0.0)
+                planes.append(jnp.concatenate([upper, lower], 0))
+            arrays.append(jnp.stack(planes))
+        return arrays
 
     def within(place, axis, size):
         place = place + me[axis] * size
@@ -289,7 +308,7 @@
     inside = inside & within(zl, 2, bz // 2)
     mid[0] = jnp.where(inside, relaxation / (26.0 + c1), 0.0)
     mid[1] = 27.0 + c1
-    cs1[1] = coarsened(c1)
+    cs1[...] = coarsened(c1, True)
 
     def inverse2(c2):
         shape = c2.shape
@@ -319,14 +338,18 @@
         g1 = restricted(remainder)
         f = mid[0] * g1
         mid[2] = g1
-        cs[0] = coarsened(g1 - mid[1] * f + box(f))
+        tile = coarsened(g1 - mid[1] * f + box(f), False)
+        cs[...] = jnp.where(crow < my // 4, tile, cs1[...])
         begin(make_b, near)
         hook()
         arrive(make_b, near)
-        g2 = gathered(cr, cs, 0)
-        c2 = gathered(cr1, cs1, 1)
-        inv = inverse2(c2)
-        diag = 27.0 + c2
+        if cr is cr1:
+            g2, c2 = gathered(cr, cs, (False, True))
+            kept[0] = inverse2(c2)
+            kept[1] = 27.0 + c2
+        else:
+            g2, = gathered(cr, cs, (False,))
+        inv, diag = kept[0], kept[1]
         e = inv * g2
         for sweep in range(SWEEPS - 1):
             e = e + inv * (g2 - diag * e + box(e))
@@ -397,8 +420,6 @@
     arrive(make_c, close)
     spread(zr2, 0, 2)
 
-    state = []
-
     def hook():
         line_begin(1, line_end(2))
 
@@ -406,20 +427,14 @@
         line_begin(0, line_end(1))
 
     def finish2(i, e, out):
-        if not state:
-            total = line_end(0)
-            total = jnp.sum(total, axis=1, keepdims=True)
-            state.append(total[0:1] / total[1:2])
-        alpha = state[0]
-        p, im = pre_ref[i], img_ref[i]
-        sol_ref[i] = alpha * p
-        res_ref[i] = g_ref[i] - alpha * im
-        pre_ref[i] = p - alpha * e
-        img_ref[i] = im - alpha * out
+        twice_ref[i] = e
+        image_twice_ref[i] = out
 
     make_d = lambda n, o: coarse_copy(3, n, o, cs2, cr2)
     cycle(lambda i: (im0[0, i], t1[2, i]), make_d, cs2, cr2, hook, second, finish2)
 
+    total = jnp.sum(line_end(0), axis=1, keepdims=True)
+    alpha_ref[...] = jnp.broadcast_to(total[0:1] / total[1:2], alpha_ref.shape)
     leave(make_a, close)
     leave(make_b, near)
     leave(make_c, close)
@@ -439,14 +454,15 @@
         mx, my = bx // 2 + 4, ey // 2
         qx = bx // 4
         most = (2 * kx + 1) * 9
+        planes = qx + 2 * min(PART, kx * qx)
         f32 = jnp.float32
         out = jax.ShapeDtypeStruct(block, f32)
         vmem = pl.BlockSpec(memory_space=pltpu.VMEM)
-        return tuple(pl.pallas_call(
+        precond, image, twice, image_twice, alpha = pl.pallas_call(
             functools.partial(kernel, counts, block, kx),
-            out_shape=[out] * 4,
+            out_shape=[out] * 4 + [jax.ShapeDtypeStruct((8, bz), f32)],
             in_specs=[vmem] * 2,
-            out_specs=[vmem] * 4,
+            out_specs=[vmem] * 5,
             scratch_shapes=[
                 pltpu.VMEM((2, ex, ey, bz), f32),
                 pltpu.VMEM((1, ex, ey, bz), f32),
@@ -463,10 +479,11 @@
                 pltpu.VMEM(((mx - 2) * ey, bz), f32),
                 pltpu.VMEM((qx * my, bz), f32),
                 pltpu.VMEM(((qx + 2) * my, bz), f32),
-                pltpu.VMEM((2, qx, my // 2, bz), f32),
-                pltpu.VMEM((1, qx, my // 2, bz), f32),
-                pltpu.VMEM((2 * kx + 1, 3, 3, 2, qx, my // 2, bz), f32),
-                pltpu.VMEM((2 * kx + 1, 3, 3, 1, qx, my // 2, bz), f32),
+                pltpu.VMEM((my // 2, bz), f32),
+                pltpu.VMEM((my // 2, bz), f32),
+                pltpu.VMEM((2 * kx + 1, 3, 3, my // 2, bz), f32),
+                pltpu.VMEM((2 * kx + 1, 3, 3, my // 2, bz), f32),
+                pltpu.VMEM((2, planes, my, bz), f32),
                 pltpu.VMEM((3, mx, my, bz), f32),
                 pltpu.VMEM((3, 8, bz), f32),
                 pltpu.VMEM((sum(counts), 8, bz), f32),
@@ -477,7 +494,10 @@
             ],
             compiler_params=pltpu.CompilerParams(collective_id=0, has_side_effects=True),
             name="relayed",
-        )(right_side, coefficient))
+        )(right_side, coefficient)
+        alpha = alpha[0]
+        return (alpha * precond, right_side - alpha * image,
+                precond - alpha * twice, image - alpha * image_twice)
 
     placed = (P(*AXES), P(*AXES))
     return jax.shard_map(

time: 41.5 us -> 36.3 us (0.87)
  Pallas kernels: 36.6 us -> 32.9 us
  local copies, waits for them, and re-layouts: 4.07 us -> 0.69 us
  other arithmetic: 0 us -> 1.79 us
    unnamed x10 -> x2, local copies, waits for them, and re-layouts: 4.07 us -> 0.01 us
    pallas_call x1, Pallas kernels: 36.6 us -> 32.9 us  [shards(): pl.pallas_call(functools.partial(kernel, counts, block, kx), out_shape=[o...]
    sub x0 -> x1, other arithmetic: none -> 1.79 us  [shards(): image - alpha * image_twice]
    mul x0 -> x1, local copies, waits for them, and re-layouts: none -> 0.69 us  [shards(): alpha * precond]
where the time goes in v2:
time: 36.3 us; the launch traced here: 36 us
  Pallas kernels  32.9 us (91%)
  other arithmetic  1.79 us (5%)
  local copies, waits for them, and re-layouts  0.69 us (2%)
  between operations  0.65 us (2%)
    pallas_call x1, Pallas kernels, shards(): pl.pallas_call(functools.partial(kernel, counts, block, kx), out_shape=[o...  32.9 us
    sub x1, other arithmetic, shards(): image - alpha * image_twice  1.79 us

profile of v2, /device:TPU:0, one launch (start us, length us, event | category | flops | bytes accessed | tf_op | source)
XLA Modules:
  0.0 36.0 jit_solution(11547064205339216381)
XLA Ops:
  0.6 0.0 copy-start
  0.6 32.9 %relayed.1 = (f32[12,16,128]{2,1,0:T(8,128)}, f32[12,16,128]{2,1,0:T(8,128)}, f32[12,16,128]{2,1,0:T(8,128)}, f32[12,16,128]{2,1,0:T(8,128)}, f32[8,128]{1,0:T(8,128)}) custom-call(f32[12,16,128]{2,1,0:T(8,128)} %g_ref.1, f32[12,16,128]{2,1,0:T(8,128)} %c_ref.1), custom_call_target="tpu_custom_call" | custom-call | tf_op jit(solution)/shard_map/relayed/pallas_call | solution.py:461
  33.6 0.7 %slice_bitcast_fusion = f32[128]{0:T(128)S(1)} fusion(f32[8,128]{1,0:T(8,128)} %get-tuple-element.9), kind=kLoop, calls=%fused_computation.4 | loop fusion | bytes 1024 | tf_op jit(solution)/shard_map/mul | solution.py:499
  34.2 0.0 copy-done
  34.3 1.8 %multiply_subtract_fusion = (f32[12,16,128]{2,1,0:T(8,128)}, f32[12,16,128]{2,1,0:T(8,128)}, f32[12,16,128]{2,1,0:T(8,128)}, f32[12,16,128]{2,1,0:T(8,128)}) fusion(f32[12,16,128]{2,1,0:T(8,128)} %get-tuple-element.11, f32[12,16,128]{2,1,0:T(8,128)} %get-tuple-element.13, f32[128]{0:T(128)S(1)} %slice_bitcast_fusion, f32[12,16,128]{2,1,0:T(8,128)S(1)} %copy-done, ...), kind=kLoop, calls=%fused_computation | loop fusion | flops 172032 | bytes 885248 | tf_op jit(solution)/shard_map/sub | solution.py:500
Async XLA Ops:
  0.6 33.6 %copy-start = (f32[12,16,128]{2,1,0:T(8,128)S(1)}, f32[12,16,128]{2,1,0:T(8,128)}, u32[]{:S(2)}) copy-start(f32[12,16,128]{2,1,0:T(8,128)} %g_ref.1) | copy-start | bytes 294916

commit v3 on v2

--- a/solution.py
+++ b/solution.py
@@ -69,11 +69,8 @@
             lines.append((axis, step, tuple(to)))
 
     zr1[...] = jnp.zeros_like(zr1)
-    zr2[...] = jnp.zeros_like(zr2)
     gc0[...] = jnp.zeros_like(gc0)
-    im0[...] = jnp.zeros_like(im0)
     cr1[...] = jnp.zeros_like(cr1)
-    cr2[...] = jnp.zeros_like(cr2)
 
     for offset in near:
         @pl.when(valid(offset))
@@ -286,6 +283,8 @@
     g = [g_ref[i] for i in range(bx)]
     fill(gc0, pk1, 0, g)
     fill(gc0, pk1, 1, [c_ref[i] for i in range(bx)])
+    for buf in (zr2, im0, cr2):
+        buf[...] = jnp.zeros_like(buf)
     pl.semaphore_wait(barrier, greeted)
     make_a = lambda n, o: fine_copy(0, n, o, gc0, pk1, zr1)
     begin(make_a, close)
@@ -460,7 +459,7 @@
         vmem = pl.BlockSpec(memory_space=pltpu.VMEM)
         precond, image, twice, image_twice, alpha = pl.pallas_call(
             functools.partial(kernel, counts, block, kx),
-            out_shape=[out] * 4 + [jax.ShapeDtypeStruct((8, bz), f32)],
+            out_shape=[out] * 4 + [jax.ShapeDtypeStruct((1, 1, bz), f32)],
             in_specs=[vmem] * 2,
             out_specs=[vmem] * 5,
             scratch_shapes=[
@@ -495,7 +494,6 @@
             compiler_params=pltpu.CompilerParams(collective_id=0, has_side_effects=True),
             name="relayed",
         )(right_side, coefficient)
-        alpha = alpha[0]
         return (alpha * precond, right_side - alpha * image,
                 precond - alpha * twice, image - alpha * image_twice)
 

time: 36.3 us -> 36.2 us (level)
    mul x1 -> x0, local copies, waits for them, and re-layouts: 0.69 us -> none  [shards(): alpha * precond]
    unnamed x2 -> x4, local copies, waits for them, and re-layouts: 0.01 us -> 0.65 us
where the time goes in v3:
time: 36.2 us; the launch traced here: 36 us
  Pallas kernels  32.9 us (91%)
  other arithmetic  1.78 us (5%)
  between operations  0.66 us (2%)
  local copies, waits for them, and re-layouts  0.65 us (2%)
    pallas_call x1, Pallas kernels, shards(): pl.pallas_call(functools.partial(kernel, counts, block, kx), out_shape=[o...  32.9 us
    sub x1, other arithmetic, shards(): image - alpha * image_twice  1.78 us

profile of v3, /device:TPU:0, one launch (start us, length us, event | category | flops | bytes accessed | tf_op | source)
XLA Modules:
  0.0 36.0 jit_solution(6003137607642590870)
XLA Ops:
  0.6 0.0 copy-start
  0.6 32.9 %relayed.1 = (f32[12,16,128]{2,1,0:T(8,128)}, f32[12,16,128]{2,1,0:T(8,128)}, f32[12,16,128]{2,1,0:T(8,128)}, f32[12,16,128]{2,1,0:T(8,128)}, f32[1,1,128]{2,1,0:T(1,128)}) custom-call(f32[12,16,128]{2,1,0:T(8,128)} %g_ref.1, f32[12,16,128]{2,1,0:T(8,128)} %c_ref.1), custom_call_target="tpu_custom_call" | custom-call | tf_op jit(solution)/shard_map/relayed/pallas_call | solution.py:460
  33.5 0.0 copy-start.1
  33.5 0.0 copy-done
  33.5 0.6 %copy-done.1 = f32[1,1,128]{2,1,0:T(1,128)S(1)} copy-done((f32[1,1,128]{2,1,0:T(1,128)S(1)}, f32[1,1,128]{2,1,0:T(1,128)}, u32[]{:S(2)}) %copy-start.1) | copy-done | bytes 536
  34.2 1.8 %multiply_subtract_fusion = (f32[12,16,128]{2,1,0:T(8,128)}, f32[12,16,128]{2,1,0:T(8,128)}, f32[12,16,128]{2,1,0:T(8,128)}, f32[12,16,128]{2,1,0:T(8,128)}) fusion(f32[12,16,128]{2,1,0:T(8,128)} %get-tuple-element.11, f32[12,16,128]{2,1,0:T(8,128)} %get-tuple-element.13, f32[128]{0:T(128)S(1)} %bitcast.1, f32[12,16,128]{2,1,0:T(8,128)S(1)} %copy-done, ...), kind=kLoop, calls=%fused_computation | loop fusion | flops 172032 | bytes 885248 | tf_op jit(solution)/shard_map/sub | solution.py:498
Async XLA Ops:
  0.6 32.9 %copy-start = (f32[12,16,128]{2,1,0:T(8,128)S(1)}, f32[12,16,128]{2,1,0:T(8,128)}, u32[]{:S(2)}) copy-start(f32[12,16,128]{2,1,0:T(8,128)} %g_ref.1) | copy-start | bytes 294916
  33.5 0.7 %copy-start.1 = (f32[1,1,128]{2,1,0:T(1,128)S(1)}, f32[1,1,128]{2,1,0:T(1,128)}, u32[]{:S(2)}) copy-start(f32[1,1,128]{2,1,0:T(1,128)} %get-tuple-element.9) | copy-start | bytes 1540
